TPU v7x, 32 devices: a 4x2x2 block of a 4x4x8 slice. The times are simulated.
32 devices in a mesh: dp: 4 (over y, z), sp: 8 (over x, core).
Axes of the slice: x: 4, y: 2, z: 2, core: 2. Of those that a mesh axis runs over, the one named last changes fastest.
The devices are a block of a 4x4x8 slice.
Arguments:
- images: bfloat16 [128, 32, 512, 64], P('dp', 'sp'), parts along dimension 0
- w_a: bfloat16 [1, 3, 3, 64, 64], replicated
- bn_a: float32 [1, 2, 64], replicated
- w_down: bfloat16 [3, 3, 64, 128], replicated
- bn_down: float32 [2, 128], replicated
- w_in: bfloat16 [3, 128, 128], replicated
- bn_in: float32 [3, 2, 128], replicated
- w_mid: bfloat16 [3, 3, 3, 128, 128], replicated
- bn_mid: float32 [3, 2, 128], replicated
- w_out: bfloat16 [3, 128, 128], replicated
- bn_out: float32 [3, 2, 128], replicated
Outputs:
- output: bfloat16 [128, 16, 256, 128], P('dp', 'sp'), parts along dimension 0
There are 4 independent parts. A program takes and returns all parts, laid end to end along the dimension named above; an argument that names none is the same for every part.
All inputs are finite; a program needn't handle non-finite values.
Results may differ from a plain program's by a relative error of at most 0.0193321.
Values are sent between devices in bfloat16 or wider.
A program may use at most 768 MiB of HBM per device.

v0:
```python
import jax
import jax.numpy as jnp
from jax import lax
from jax.sharding import PartitionSpec as P, NamedSharding

NORM_EPS = 1e-5
CONV_DIMS = ("NHWC", "HWIO", "NHWC")


def solution(mesh):
    groups = mesh.shape["sp"]
    to_next = [(device, device + 1) for device in range(groups - 1)]
    to_prev = [(device + 1, device) for device in range(groups - 1)]

    def conv_same(hidden, weight):
        from_above = lax.ppermute(hidden[:, -1:], "sp", to_next)
        from_below = lax.ppermute(hidden[:, :1], "sp", to_prev)
        padded = jnp.concatenate([from_above, hidden, from_below], axis=1)
        return lax.conv_general_dilated(padded, weight, (1, 1), ((0, 0), (1, 1)), dimension_numbers=CONV_DIMS, preferred_element_type=jnp.float32)

    def conv_down(hidden, weight):
        from_below = lax.ppermute(hidden[:, :1], "sp", to_prev)
        padded = jnp.concatenate([hidden, from_below], axis=1)
        return lax.conv_general_dilated(padded, weight, (2, 2), ((0, 0), (0, 1)), dimension_numbers=CONV_DIMS, preferred_element_type=jnp.float32)

    def conv_point(hidden, weight):
        return jnp.einsum("bhwc,cd->bhwd", hidden, weight, preferred_element_type=jnp.float32)

    def batch_norm(pre_act, params):
        norm_count = pre_act.shape[0] * pre_act.shape[1] * pre_act.shape[2] * groups
        part_sums = jnp.stack([jnp.sum(pre_act, axis=(0, 1, 2)), jnp.sum(pre_act * pre_act, axis=(0, 1, 2))])
        group_moments = lax.psum(part_sums, "sp") / norm_count
        chan_mean = group_moments[0]
        chan_var = group_moments[1] - chan_mean * chan_mean
        chan_scale = params[0] * lax.rsqrt(chan_var + NORM_EPS)
        return (pre_act - chan_mean) * chan_scale + params[1]

    def norm_relu(pre_act, params):
        return jax.nn.relu(batch_norm(pre_act, params)).astype(jnp.bfloat16)

    def forward(images, w_a, bn_a, w_down, bn_down, w_in, bn_in, w_mid, bn_mid, w_out, bn_out):
        hidden = images
        for layer_num in range(w_a.shape[0]):
            hidden = norm_relu(conv_same(hidden, w_a[layer_num]), bn_a[layer_num])
        hidden = norm_relu(conv_down(hidden, w_down), bn_down)
        for block_num in range(w_in.shape[0]):
            branch = norm_relu(conv_point(hidden, w_in[block_num]), bn_in[block_num])
            branch = norm_relu(conv_same(branch, w_mid[block_num]), bn_mid[block_num])
            summed = batch_norm(conv_point(branch, w_out[block_num]), bn_out[block_num]) + hidden
            hidden = jax.nn.relu(summed).astype(jnp.bfloat16)
        return hidden

    act_spec = P("dp", "sp", None, None)
    return jax.shard_map(forward, mesh=mesh, in_specs=(act_spec,) + (P(),) * 10, out_specs=act_spec, check_vma=False)
```

profile of v0, /device:TPU:81, one launch (start us, length us, event | category | flops | bytes accessed | tf_op | source)
XLA Modules:
  0.0 550.4 jit_solution(10697867241525479859)
XLA Ops:
  11.5 24.3 %copy.29 = bf16[32,4,512,64]{3,0,2,1:T(8,128)(2,1)} copy(bf16[32,4,512,64]{2,3,1,0:T(8,128)(2,1)} %param.11) | data formatting | bytes 16777216 | tf_op args[0]
  49.9 30.6 %fusion.124 = (f32[64]{0:T(128)S(1)}, f32[64]{0:T(128)S(1)}, f32[32,4,512,64]{3,0,2,1:T(8,128)}) fusion(bf16[1,3,3,64,64]{4,3,2,1,0:T(8,128)(2,1)S(1)} %copy-done, bf16[32,1,512,64]{3,0,2,1:T(8,128)(2,1)} %copy.30, bf16[32,4,512,64]{3,0,2,1:T(8,128)(2,1)} %copy.29, bf16[32,1,512,64]{3,0,2,1:T(8,128)(2,1)} %copy.28), kind=kOutput, calls=%fused_computation.201 | convolution fusion | flops 4875878400 | bytes 29434368 | tf_op jit(solution)/shard_map/conv_general_dilated | solution.py:19
  80.5 12.7 %psum.77 = f32[2,64]{1,0:T(2,128)S(1)} all-reduce(f32[2,64]{1,0:T(2,128)S(1)} %pad_maximum_fusion), channel_id=1, replica_groups=mesh['dp'=4,'sp'=8] {'sp'}, use_global_device_ids=true, to_apply=%region_2.0 | all-reduce | flops 128 | bytes 1024 | tf_op jit(solution)/shard_map/psum | solution.py:32
  93.3 13.7 %maximum_convert_fusion = bf16[32,4,512,64]{3,0,2,1:T(8,128)(2,1)S(1)} fusion(f32[32,4,512,64]{3,0,2,1:T(8,128)} %get-tuple-element.44, f32[64]{0:T(128)S(1)} %slice_bitcast_fusion.20, f32[64]{0:T(128)S(1)} %fusion.118, f32[64]{0:T(128)S(1)} %slice_bitcast_fusion.21), kind=kLoop, calls=%fused_computation | loop fusion | flops 20971520 | bytes 25166592 | tf_op jit(solution)/shard_map/convert_element_type | solution.py:39
  123.9 23.4 %collective-permute-done.2 = bf16[32,1,512,64]{2,3,1,0:T(8,128)(2,1)} collective-permute-done((bf16[32,1,512,64]{2,3,1,0:T(8,128)(2,1)S(1)}, bf16[32,1,512,64]{2,3,1,0:T(8,128)(2,1)}, u32[]{:S(2)}, u32[]{:S(2)}) %collective-permute-start.2) | collective-permute-done | bytes 2097184 | tf_op jit(solution)/shard_map/ppermute | solution.py:22
  154.7 13.1 %fusion.134 = (f32[128]{0:T(128)S(1)}, f32[128]{0:T(128)S(1)}, f32[32,2,256,128]{3,0,2,1:T(8,128)}) fusion(bf16[3,3,64,128]{3,2,1,0:T(8,128)(2,1)S(1)} %copy-done.13, bf16[32,1,512,64]{3,0,2,1:T(8,128)(2,1)} %copy.32, bf16[32,4,512,64]{3,0,2,1:T(8,128)(2,1)} %copy-done.4), kind=kOutput, calls=%fused_computation.211 | convolution fusion | flops 2440036352 | bytes 19022848 | tf_op jit(solution)/shard_map/conv_general_dilated | solution.py:24
  167.8 9.9 %psum.78 = f32[2,128]{1,0:T(2,128)S(1)} all-reduce(f32[2,128]{1,0:T(2,128)S(1)} %pad_maximum_fusion.1), channel_id=1, replica_groups=mesh['dp'=4,'sp'=8] {'sp'}, use_global_device_ids=true, to_apply=%region_5.6 | all-reduce | flops 256 | bytes 2048 | tf_op jit(solution)/shard_map/psum | solution.py:32
  182.6 7.5 %fusion.133 = (f32[128]{0:T(128)S(1)}, f32[128]{0:T(128)S(1)}, f32[32,2,256,128]{3,2,1,0:T(8,128)}) fusion(bf16[3,128,128]{2,1,0:T(8,128)(2,1)S(1)} %copy-done.5, bf16[32,2,256,128]{3,0,2,1:T(8,128)(2,1)S(1)} %maximum_convert_fusion.4), kind=kOutput, calls=%fused_computation.210 | convolution fusion | flops 543162112 | bytes 12616704 | tf_op jit(solution)/shard_map/bhwc,cd->bhwd/dot_general | solution.py:27
  190.1 15.3 %psum.79 = f32[2,128]{1,0:T(2,128)S(1)} all-reduce(f32[2,128]{1,0:T(2,128)S(1)} %pad_maximum_fusion.2), channel_id=1, replica_groups=mesh['dp'=4,'sp'=8] {'sp'}, use_global_device_ids=true, to_apply=%region_8.9 | all-reduce | flops 256 | bytes 2048 | tf_op jit(solution)/shard_map/psum | solution.py:32
  205.5 9.0 %fusion.54 = bf16[32,2,256,128]{3,0,2,1:T(8,128)(2,1)S(1)} fusion(f32[32,2,256,128]{3,2,1,0:T(8,128)} %get-tuple-element.46, f32[128]{0:T(128)S(1)} %get-tuple-element.43, f32[128]{0:T(128)S(1)} %fusion.112, f32[128]{0:T(128)S(1)} %slice_bitcast_fusion.17), kind=kLoop, calls=%fused_computation.62 | loop fusion | flops 10485760 | bytes 12584448 | tf_op jit(solution)/shard_map/convert_element_type | solution.py:39
  219.9 20.1 %collective-permute-done.3 = bf16[32,1,256,128]{3,0,2,1:T(8,128)(2,1)S(1)} collective-permute-done((bf16[32,1,256,128]{3,0,2,1:T(8,128)(2,1)S(1)}, bf16[32,1,256,128]{3,0,2,1:T(8,128)(2,1)S(1)}, u32[]{:S(2)}, u32[]{:S(2)}) %collective-permute-start.3) | collective-permute-done | bytes 2097184 | tf_op jit(solution)/shard_map/ppermute | solution.py:16
  244.5 12.5 %fusion.132 = (f32[128]{0:T(128)S(1)}, f32[128]{0:T(128)S(1)}, f32[32,2,256,128]{3,0,2,1:T(8,128)}) fusion(bf16[3,3,3,128,128]{4,3,2,1,0:T(8,128)(2,1)S(1)} %copy-done.12, bf16[32,1,256,128]{3,0,2,1:T(8,128)(2,1)S(1)} %collective-permute-done.4, bf16[32,2,256,128]{3,0,2,1:T(8,128)(2,1)S(1)} %fusion.54, bf16[32,1,256,128]{3,0,2,1:T(8,128)(2,1)S(1)} %collective-permute-done.3), kind=kOutput, calls=%fused_computation.209 | convolution fusion | flops 4850712576 | bytes 17073152 | tf_op jit(solution)/shard_map/conv_general_dilated | solution.py:19
  257.0 9.5 %psum.80 = f32[2,128]{1,0:T(2,128)S(1)} all-reduce(f32[2,128]{1,0:T(2,128)S(1)} %pad_maximum_fusion.3), channel_id=1, replica_groups=mesh['dp'=4,'sp'=8] {'sp'}, use_global_device_ids=true, to_apply=%region_11.12 | all-reduce | flops 256 | bytes 2048 | tf_op jit(solution)/shard_map/psum | solution.py:32
  271.4 7.5 %fusion.131 = (f32[128]{0:T(128)S(1)}, f32[128]{0:T(128)S(1)}, f32[32,2,256,128]{3,2,1,0:T(8,128)}) fusion(bf16[3,128,128]{2,1,0:T(8,128)(2,1)S(1)} %copy-done.6, bf16[32,2,256,128]{3,0,2,1:T(8,128)(2,1)S(1)} %maximum_convert_fusion.3), kind=kOutput, calls=%fused_computation.208 | convolution fusion | flops 543162112 | bytes 12616704 | tf_op jit(solution)/shard_map/bhwc,cd->bhwd/dot_general | solution.py:27
  278.9 15.5 %psum.81 = f32[2,128]{1,0:T(2,128)S(1)} all-reduce(f32[2,128]{1,0:T(2,128)S(1)} %pad_maximum_fusion.4), channel_id=1, replica_groups=mesh['dp'=4,'sp'=8] {'sp'}, use_global_device_ids=true, to_apply=%region_14.15 | all-reduce | flops 256 | bytes 2048 | tf_op jit(solution)/shard_map/psum | solution.py:32
  294.5 10.1 %fusion.50 = bf16[32,2,256,128]{3,0,2,1:T(8,128)(2,1)S(1)} fusion(f32[32,2,256,128]{3,2,1,0:T(8,128)} %get-tuple-element.48, f32[128]{0:T(128)S(1)} %get-tuple-element.37, f32[128]{0:T(128)S(1)} %fusion.106, f32[128]{0:T(128)S(1)} %slice_bitcast_fusion.13, f32[128]{0:T(128)S(1)} %slice_bitcast_fusion.18, f32[128]{0:T(128)S(1)} %fusion.115, ...), kind=kLoop, calls=%fused_computation.57 | loop fusion | flops 25165824 | bytes 20974592 | tf_op jit(solution)/shard_map/convert_element_type | solution.py:50
  314.1 12.8 %psum.82 = f32[2,128]{1,0:T(2,128)S(1)} all-reduce(f32[2,128]{1,0:T(2,128)S(1)} %pad_maximum_fusion.5), channel_id=1, replica_groups=mesh['dp'=4,'sp'=8] {'sp'}, use_global_device_ids=true, to_apply=%region_17.18 | all-reduce | flops 256 | bytes 2048 | tf_op jit(solution)/shard_map/psum | solution.py:32
  326.9 8.9 %fusion.45 = bf16[32,2,256,128]{3,0,2,1:T(8,128)(2,1)S(1)} fusion(f32[32,2,256,128]{3,2,1,0:T(8,128)} %get-tuple-element.49, f32[128]{0:T(128)S(1)} %get-tuple-element.42, f32[128]{0:T(128)S(1)} %fusion.103, f32[128]{0:T(128)S(1)} %slice_bitcast_fusion.11), kind=kLoop, calls=%fused_computation.51 | loop fusion | flops 10485760 | bytes 12584448 | tf_op jit(solution)/shard_map/convert_element_type | solution.py:39
  341.1 20.4 %collective-permute-done.5 = bf16[32,1,256,128]{3,0,2,1:T(8,128)(2,1)S(1)} collective-permute-done((bf16[32,1,256,128]{3,0,2,1:T(8,128)(2,1)S(1)}, bf16[32,1,256,128]{3,0,2,1:T(8,128)(2,1)S(1)}, u32[]{:S(2)}, u32[]{:S(2)}) %collective-permute-start.5) | collective-permute-done | bytes 2097184 | tf_op jit(solution)/shard_map/ppermute | solution.py:16
  365.9 12.5 %fusion.129 = (f32[128]{0:T(128)S(1)}, f32[128]{0:T(128)S(1)}, f32[32,2,256,128]{3,0,2,1:T(8,128)}) fusion(bf16[3,3,3,128,128]{4,3,2,1,0:T(8,128)(2,1)S(1)} %copy-done.12, bf16[32,1,256,128]{3,0,2,1:T(8,128)(2,1)S(1)} %collective-permute-done.6, bf16[32,2,256,128]{3,0,2,1:T(8,128)(2,1)S(1)} %fusion.45, bf16[32,1,256,128]{3,0,2,1:T(8,128)(2,1)S(1)} %collective-permute-done.5), kind=kOutput, calls=%fused_computation.206 | convolution fusion | flops 4850712576 | bytes 17073152 | tf_op jit(solution)/shard_map/conv_general_dilated | solution.py:19
  378.4 9.9 %psum.83 = f32[2,128]{1,0:T(2,128)S(1)} all-reduce(f32[2,128]{1,0:T(2,128)S(1)} %pad_maximum_fusion.6), channel_id=1, replica_groups=mesh['dp'=4,'sp'=8] {'sp'}, use_global_device_ids=true, to_apply=%region_20.21 | all-reduce | flops 256 | bytes 2048 | tf_op jit(solution)/shard_map/psum | solution.py:32
  393.2 7.5 %fusion.128 = (f32[128]{0:T(128)S(1)}, f32[128]{0:T(128)S(1)}, f32[32,2,256,128]{3,2,1,0:T(8,128)}) fusion(bf16[3,128,128]{2,1,0:T(8,128)(2,1)S(1)} %copy-done.6, bf16[32,2,256,128]{3,0,2,1:T(8,128)(2,1)S(1)} %maximum_convert_fusion.2), kind=kOutput, calls=%fused_computation.205 | convolution fusion | flops 543162112 | bytes 12616704 | tf_op jit(solution)/shard_map/bhwc,cd->bhwd/dot_general | solution.py:27
  400.7 15.5 %psum.84 = f32[2,128]{1,0:T(2,128)S(1)} all-reduce(f32[2,128]{1,0:T(2,128)S(1)} %pad_maximum_fusion.7), channel_id=1, replica_groups=mesh['dp'=4,'sp'=8] {'sp'}, use_global_device_ids=true, to_apply=%region_23.24 | all-reduce | flops 256 | bytes 2048 | tf_op jit(solution)/shard_map/psum | solution.py:32
  416.2 9.4 %fusion.41 = bf16[32,2,256,128]{3,0,2,1:T(8,128)(2,1)S(1)} fusion(f32[32,2,256,128]{3,2,1,0:T(8,128)} %get-tuple-element.51, bf16[32,2,256,128]{3,0,2,1:T(8,128)(2,1)} %copy-done.3, f32[128]{0:T(128)S(1)} %get-tuple-element.36, f32[128]{0:T(128)S(1)} %fusion.97, f32[128]{0:T(128)S(1)} %slice_bitcast_fusion.7), kind=kLoop, calls=%fused_computation.46 | loop fusion | flops 14680064 | bytes 16778752 | tf_op jit(solution)/shard_map/convert_element_type | solution.py:50
  435.2 12.7 %psum.85 = f32[2,128]{1,0:T(2,128)S(1)} all-reduce(f32[2,128]{1,0:T(2,128)S(1)} %pad_maximum_fusion.8), channel_id=1, replica_groups=mesh['dp'=4,'sp'=8] {'sp'}, use_global_device_ids=true, to_apply=%region_26.27 | all-reduce | flops 256 | bytes 2048 | tf_op jit(solution)/shard_map/psum | solution.py:32
  448.0 8.9 %fusion.36 = bf16[32,2,256,128]{3,0,2,1:T(8,128)(2,1)S(1)} fusion(f32[32,2,256,128]{3,2,1,0:T(8,128)} %get-tuple-element.52, f32[128]{0:T(128)S(1)} %get-tuple-element.41, f32[128]{0:T(128)S(1)} %fusion.94, f32[128]{0:T(128)S(1)} %slice_bitcast_fusion.5), kind=kLoop, calls=%fused_computation.40 | loop fusion | flops 10485760 | bytes 12584448 | tf_op jit(solution)/shard_map/convert_element_type | solution.py:39
  462.1 20.4 %collective-permute-done.7 = bf16[32,1,256,128]{3,0,2,1:T(8,128)(2,1)S(1)} collective-permute-done((bf16[32,1,256,128]{3,0,2,1:T(8,128)(2,1)S(1)}, bf16[32,1,256,128]{3,0,2,1:T(8,128)(2,1)S(1)}, u32[]{:S(2)}, u32[]{:S(2)}) %collective-permute-start.7) | collective-permute-done | bytes 2097184 | tf_op jit(solution)/shard_map/ppermute | solution.py:16
  486.9 12.5 %fusion.126 = (f32[128]{0:T(128)S(1)}, f32[128]{0:T(128)S(1)}, f32[32,2,256,128]{3,0,2,1:T(8,128)}) fusion(bf16[3,3,3,128,128]{4,3,2,1,0:T(8,128)(2,1)S(1)} %copy-done.12, bf16[32,1,256,128]{3,0,2,1:T(8,128)(2,1)S(1)} %collective-permute-done.8, bf16[32,2,256,128]{3,0,2,1:T(8,128)(2,1)S(1)} %fusion.36, bf16[32,1,256,128]{3,0,2,1:T(8,128)(2,1)S(1)} %collective-permute-done.7), kind=kOutput, calls=%fused_computation.203 | convolution fusion | flops 4850712576 | bytes 17073152 | tf_op jit(solution)/shard_map/conv_general_dilated | solution.py:19
  499.4 9.7 %psum.86 = f32[2,128]{1,0:T(2,128)S(1)} all-reduce(f32[2,128]{1,0:T(2,128)S(1)} %pad_maximum_fusion.9), channel_id=1, replica_groups=mesh['dp'=4,'sp'=8] {'sp'}, use_global_device_ids=true, to_apply=%region_29.30 | all-reduce | flops 256 | bytes 2048 | tf_op jit(solution)/shard_map/psum | solution.py:32
  514.0 7.5 %fusion.125 = (f32[128]{0:T(128)S(1)}, f32[128]{0:T(128)S(1)}, f32[32,2,256,128]{3,2,1,0:T(8,128)}) fusion(bf16[3,128,128]{2,1,0:T(8,128)(2,1)S(1)} %copy-done.6, bf16[32,2,256,128]{3,0,2,1:T(8,128)(2,1)S(1)} %maximum_convert_fusion.1), kind=kOutput, calls=%fused_computation.202 | convolution fusion | flops 543162112 | bytes 12616704 | tf_op jit(solution)/shard_map/bhwc,cd->bhwd/dot_general | solution.py:27
  521.6 15.3 %psum.87 = f32[2,128]{1,0:T(2,128)S(1)} all-reduce(f32[2,128]{1,0:T(2,128)S(1)} %pad_maximum_fusion.10), channel_id=1, replica_groups=mesh['dp'=4,'sp'=8] {'sp'}, use_global_device_ids=true, to_apply=%region_32.33 | all-reduce | flops 256 | bytes 2048 | tf_op jit(solution)/shard_map/psum | solution.py:32
  536.9 9.5 %fusion.32 = bf16[32,2,256,128]{3,0,2,1:T(8,128)(2,1)S(1)} fusion(f32[32,2,256,128]{3,2,1,0:T(8,128)} %get-tuple-element.54, bf16[32,2,256,128]{3,0,2,1:T(8,128)(2,1)} %copy-done.2, f32[128]{0:T(128)S(1)} %get-tuple-element.35, f32[128]{0:T(128)S(1)} %fusion.88, f32[128]{0:T(128)S(1)} %slice_bitcast_fusion.1), kind=kLoop, calls=%fused_computation.35 | loop fusion | flops 14680064 | bytes 16778752 | tf_op jit(solution)/shard_map/convert_element_type | solution.py:50
  (107 shorter events, 121.5 us)
Async XLA Ops:
  0.0 49.9 %copy-start = (bf16[1,3,3,64,64]{4,3,2,1,0:T(8,128)(2,1)S(1)}, bf16[1,3,3,64,64]{4,3,2,1,0:T(8,128)(2,1)}, u32[]{:S(2)}) copy-start(bf16[1,3,3,64,64]{4,3,2,1,0:T(8,128)(2,1)} %param.12) | copy-start | bytes 221188
  4.8 31.0 %collective-permute-start = (bf16[32,1,512,64]{2,3,1,0:T(8,128)(2,1)}, bf16[32,1,512,64]{2,3,1,0:T(8,128)(2,1)}, u32[]{:S(2)}, u32[]{:S(2)}) collective-permute-start(bf16[32,1,512,64]{2,3,1,0:T(8,128)(2,1)} %get-tuple-element.27), channel_id=1, source_target_pairs={{0,1},{1,2},{2,3},{3,4},{4,5},{5,6},{6,7},{8,9},{9,10},{10,11},{11... | collective-permute-start | bytes 6291464 | tf_op jit(solution)/shard_map/ppermute | solution.py:16
  9.4 26.4 %copy-start.10 = (f32[1,2,64]{2,1,0:T(2,128)S(1)}, f32[1,2,64]{2,1,0:T(2,128)}, u32[]{:S(2)}) copy-start(f32[1,2,64]{2,1,0:T(2,128)} %param.13) | copy-start | bytes 1540
  9.4 33.8 %collective-permute-start.1 = (bf16[32,1,512,64]{2,3,1,0:T(8,128)(2,1)}, bf16[32,1,512,64]{2,3,1,0:T(8,128)(2,1)S(1)}, u32[]{:S(2)}, u32[]{:S(2)}) collective-permute-start(bf16[32,1,512,64]{2,3,1,0:T(8,128)(2,1)} %get-tuple-element.28), channel_id=1, source_target_pairs={{1,0},{2,1},{3,2},{4,3},{5,4},{6,5},{7,6},{9,8},{10,9},{11,10},{12... | collective-permute-start | bytes 6291464 | tf_op jit(solution)/shard_map/ppermute | solution.py:17
  107.0 5.7 %copy-start.4 = (bf16[32,4,512,64]{3,0,2,1:T(8,128)(2,1)}, bf16[32,4,512,64]{3,0,2,1:T(8,128)(2,1)S(1)}, u32[]{:S(2)}) copy-start(bf16[32,4,512,64]{3,0,2,1:T(8,128)(2,1)S(1)} %maximum_convert_fusion) | copy-start | bytes 25165828
  112.7 11.2 %copy-start.11 = (f32[2,128]{1,0:T(2,128)S(1)}, f32[2,128]{1,0:T(2,128)}, u32[]{:S(2)}) copy-start(f32[2,128]{1,0:T(2,128)} %param.15) | copy-start | bytes 3076
  112.7 11.2 %copy-start.7 = (f32[3,2,128]{2,1,0:T(2,128)S(1)}, f32[3,2,128]{2,1,0:T(2,128)}, u32[]{:S(2)}) copy-start(f32[3,2,128]{2,1,0:T(2,128)} %param.17) | copy-start | bytes 9220
  115.4 39.3 %copy-start.13 = (bf16[3,3,64,128]{3,2,1,0:T(8,128)(2,1)S(1)}, bf16[3,3,64,128]{3,2,1,0:T(8,128)(2,1)}, u32[]{:S(2)}) copy-start(bf16[3,3,64,128]{3,2,1,0:T(8,128)(2,1)} %param.14) | copy-start | bytes 442372
  119.9 27.4 %collective-permute-start.2 = (bf16[32,1,512,64]{2,3,1,0:T(8,128)(2,1)S(1)}, bf16[32,1,512,64]{2,3,1,0:T(8,128)(2,1)}, u32[]{:S(2)}, u32[]{:S(2)}) collective-permute-start(bf16[32,1,512,64]{2,3,1,0:T(8,128)(2,1)S(1)} %copy.31), channel_id=1, source_target_pairs={{1,0},{2,1},{3,2},{4,3},{5,4},{6,5},{7,6},{9,8},{10,9},{11,10},{12... | collective-permute-start | bytes 6291464 | tf_op jit(solution)/shard_map/ppermute | solution.py:22
  167.8 14.8 %copy-start.5 = (bf16[3,128,128]{2,1,0:T(8,128)(2,1)S(1)}, bf16[3,128,128]{2,1,0:T(8,128)(2,1)}, u32[]{:S(2)}) copy-start(bf16[3,128,128]{2,1,0:T(8,128)(2,1)} %param.16) | copy-start | bytes 294916
  205.4 14.5 %copy-start.8 = (f32[3,2,128]{2,1,0:T(2,128)S(1)}, f32[3,2,128]{2,1,0:T(2,128)}, u32[]{:S(2)}) copy-start(f32[3,2,128]{2,1,0:T(2,128)} %param.19) | copy-start | bytes 9220
  205.4 14.5 %copy-start.9 = (f32[3,2,128]{2,1,0:T(2,128)S(1)}, f32[3,2,128]{2,1,0:T(2,128)}, u32[]{:S(2)}) copy-start(f32[3,2,128]{2,1,0:T(2,128)} %param.21) | copy-start | bytes 9220
  205.4 39.1 %copy-start.12 = (bf16[3,3,3,128,128]{4,3,2,1,0:T(8,128)(2,1)S(1)}, bf16[3,3,3,128,128]{4,3,2,1,0:T(8,128)(2,1)}, u32[]{:S(2)}) copy-start(bf16[3,3,3,128,128]{4,3,2,1,0:T(8,128)(2,1)} %param.18) | copy-start | bytes 2654212
  215.2 24.9 %collective-permute-start.3 = (bf16[32,1,256,128]{3,0,2,1:T(8,128)(2,1)S(1)}, bf16[32,1,256,128]{3,0,2,1:T(8,128)(2,1)S(1)}, u32[]{:S(2)}, u32[]{:S(2)}) collective-permute-start(bf16[32,1,256,128]{3,0,2,1:T(8,128)(2,1)S(1)} %get-tuple-element.33), channel_id=1, source_target_pairs={{0,1},{1,2},{2,3},{3,4},{4,5},{5,6},{6,7},{8,9},{9,10},{10,11},{11... | collective-permute-start | bytes 6291464 | tf_op jit(solution)/shard_map/ppermute | solution.py:16
  217.1 27.4 %collective-permute-start.4 = (bf16[32,1,256,128]{3,0,2,1:T(8,128)(2,1)S(1)}, bf16[32,1,256,128]{3,0,2,1:T(8,128)(2,1)S(1)}, u32[]{:S(2)}, u32[]{:S(2)}) collective-permute-start(bf16[32,1,256,128]{3,0,2,1:T(8,128)(2,1)S(1)} %get-tuple-element.34), channel_id=1, source_target_pairs={{1,0},{2,1},{3,2},{4,3},{5,4},{6,5},{7,6},{9,8},{10,9},{11,10},{12... | collective-permute-start | bytes 6291464 | tf_op jit(solution)/shard_map/ppermute | solution.py:17
  257.0 14.4 %copy-start.6 = (bf16[3,128,128]{2,1,0:T(8,128)(2,1)S(1)}, bf16[3,128,128]{2,1,0:T(8,128)(2,1)}, u32[]{:S(2)}) copy-start(bf16[3,128,128]{2,1,0:T(8,128)(2,1)} %param.20) | copy-start | bytes 294916
  304.6 2.0 copy-start.3
  336.6 24.9 %collective-permute-start.5 = (bf16[32,1,256,128]{3,0,2,1:T(8,128)(2,1)S(1)}, bf16[32,1,256,128]{3,0,2,1:T(8,128)(2,1)S(1)}, u32[]{:S(2)}, u32[]{:S(2)}) collective-permute-start(bf16[32,1,256,128]{3,0,2,1:T(8,128)(2,1)S(1)} %get-tuple-element.31), channel_id=1, source_target_pairs={{0,1},{1,2},{2,3},{3,4},{4,5},{5,6},{6,7},{8,9},{9,10},{10,11},{11... | collective-permute-start | bytes 6291464 | tf_op jit(solution)/shard_map/ppermute | solution.py:16
  338.5 27.4 %collective-permute-start.6 = (bf16[32,1,256,128]{3,0,2,1:T(8,128)(2,1)S(1)}, bf16[32,1,256,128]{3,0,2,1:T(8,128)(2,1)S(1)}, u32[]{:S(2)}, u32[]{:S(2)}) collective-permute-start(bf16[32,1,256,128]{3,0,2,1:T(8,128)(2,1)S(1)} %get-tuple-element.32), channel_id=1, source_target_pairs={{1,0},{2,1},{3,2},{4,3},{5,4},{6,5},{7,6},{9,8},{10,9},{11,10},{12... | collective-permute-start | bytes 6291464 | tf_op jit(solution)/shard_map/ppermute | solution.py:17
  425.7 2.0 copy-start.2
  457.6 24.9 %collective-permute-start.7 = (bf16[32,1,256,128]{3,0,2,1:T(8,128)(2,1)S(1)}, bf16[32,1,256,128]{3,0,2,1:T(8,128)(2,1)S(1)}, u32[]{:S(2)}, u32[]{:S(2)}) collective-permute-start(bf16[32,1,256,128]{3,0,2,1:T(8,128)(2,1)S(1)} %get-tuple-element.29), channel_id=1, source_target_pairs={{0,1},{1,2},{2,3},{3,4},{4,5},{5,6},{6,7},{8,9},{9,10},{10,11},{11... | collective-permute-start | bytes 6291464 | tf_op jit(solution)/shard_map/ppermute | solution.py:16
  459.6 27.4 %collective-permute-start.8 = (bf16[32,1,256,128]{3,0,2,1:T(8,128)(2,1)S(1)}, bf16[32,1,256,128]{3,0,2,1:T(8,128)(2,1)S(1)}, u32[]{:S(2)}, u32[]{:S(2)}) collective-permute-start(bf16[32,1,256,128]{3,0,2,1:T(8,128)(2,1)S(1)} %get-tuple-element.30), channel_id=1, source_target_pairs={{1,0},{2,1},{3,2},{4,3},{5,4},{6,5},{7,6},{9,8},{10,9},{11,10},{12... | collective-permute-start | bytes 6291464 | tf_op jit(solution)/shard_map/ppermute | solution.py:17
  536.9 13.1 %copy-start.1 = (bf16[1,3,3,64,64]{4,3,2,1,0:T(8,128)(2,1)S(1)}, bf16[1,3,3,64,64]{4,3,2,1,0:T(8,128)(2,1)}, u32[]{:S(2)}) copy-start(bf16[1,3,3,64,64]{4,3,2,1,0:T(8,128)(2,1)} %param.12) | copy-start | bytes 221188
where the time goes:
time: 561 us; the launch traced here: 550 us
  blocking collectives  139 us (25%)
  matrix products  126 us (22%)
  waiting for transfers between devices  97.6 us (17%)
  other arithmetic  89.1 us (16%)
  local copies, waits for them, and re-layouts  73.4 us (13%)
  starting transfers between devices  24.3 us (4%)
    psum x11, blocking collectives, batch_norm(): group_moments = lax.psum(part_sums, 'sp') / norm_count  139 us
    conv_general_dilated x4, matrix products, conv_same(): lax.conv_general_dilated(padded, weight, (1, 1), ((0, 0), (1, 1)), dimens...  68 us
    ppermute x4, waiting for transfers between devices, conv_same(): from_above = lax.ppermute(hidden[:, -1:], 'sp', to_next)  60.9 us
    convert_element_type x8, other arithmetic, norm_relu(): return jax.nn.relu(batch_norm(pre_act, params)).astype(jnp.bfloat16)  59.8 us
    dot_general x6, matrix products, conv_point(): jnp.einsum('bhwc,cd->bhwd', hidden, weight, preferred_element_type=jnp.fl...  45.2 us
    unnamed x29, local copies, waits for them, and re-layouts  34.1 us
    convert_element_type x3, other arithmetic, forward(): hidden = jax.nn.relu(summed).astype(jnp.bfloat16)  29 us
    ppermute x1, waiting for transfers between devices, conv_down(): from_below = lax.ppermute(hidden[:, :1], 'sp', to_prev)  23.4 us
  transfers between devices with their start and end apart: 9, of which 7 were waited for; matrix products, arithmetic and copies ran while one was open for 6% of the time, Pallas kernels for 0%

commit v1 on v0

v1 whole, which is shorter than its diff:
```python
import functools

import jax
import jax.numpy as jnp
from jax import lax
from jax.experimental import pallas as pl
from jax.experimental.pallas import tpu as pltpu
from jax.sharding import PartitionSpec as P

NORM_EPS = 1e-5
BF = jnp.bfloat16
F32 = jnp.float32
OPP_CORE = 0
GROUP = 4
SLOTS = 4


def cat(parts, axis):
    return jnp.concatenate(parts, axis=axis)


def banded(taps, rows_in, rows_out, stride, first):
    zero = jnp.zeros_like(taps[0])
    rows = []
    for ri in rows_in:
        cols = []
        for ro in rows_out:
            dy = ri + first - stride * ro
            cols.append(taps[dy] if 0 <= dy < len(taps) else zero)
        rows.append(cat(cols, 1))
    return cat(rows, 0)


def pack_weights(w_a, w_down, w_in, w_mid, w_out):
    blocks = w_in.shape[0]
    wa, w4, wdn, wdh = [], [], [], []
    for dx in range(3):
        ta = [w_a[0, dy, dx] for dy in range(3)]
        zero = jnp.zeros_like(ta[0])
        wa.append(banded(ta, range(6), range(4), 1, 0))
        w4.append(cat([cat([t, zero], 1) for t in ta + [zero]], 0))
        td = [w_down[dy, dx] for dy in range(3)]
        wdn.append(banded(td, range(4), range(2), 2, 0))
        wdh.append(banded(td + [jnp.zeros_like(td[0])], (4, 5), (0, 1), 2, 0))
    wa, w4, wd = cat(wa, 0), cat(w4, 0), cat(wdn + wdh, 0)

    def diag(w):
        z = jnp.zeros_like(w)
        return cat([cat([w, z], 1), cat([z, w], 1)], 0)

    w_in2 = jnp.stack([diag(w_in[j]) for j in range(blocks)])
    w_out2 = jnp.stack([diag(w_out[j]) for j in range(blocks)])
    loc, halo = [], []
    for j in range(blocks):
        ml, mh = [], []
        for dx in range(3):
            tm = [w_mid[j, dy, dx] for dy in range(3)]
            z = jnp.zeros_like(tm[0])
            ml.append(banded(tm, (0, 1), (0, 1), 1, 1))
            mh.append(cat([cat([tm[0], z], 1), cat([z, tm[2]], 1)], 0))
        loc.append(cat(ml, 0))
        halo.append(cat(mh, 0))
    return wa, w4, wd, w_in2, w_out2, jnp.stack(loc), jnp.stack(halo)


def body(
    dims, img, wa, w4, wd, w_in, w_out, w_loc, w_halo, bn, out,
    xb, halo, xs, za, z4, zb, hb, ub, hh, rb,
    msg, pslot, cmsg, slots,
    ld_sem, im_send, im_recv, ex_send, ex_recv, ar_send, ar_recv, out_sem,
):
    n_img, width, sp_n, blocks, count_a, count_b = dims
    half = width // 2
    n_grp = n_img // GROUP
    rows = GROUP * half
    me = lax.axis_index("sp")
    core = lax.rem(me, 2)
    chip = lax.div(me, 2)
    chips = sp_n // 2
    has_up = me > 0
    has_dn = me < sp_n - 1
    up = jnp.maximum(me - 1, 0)
    dn = jnp.minimum(me + 1, sp_n - 1)

    def remote(src, dst, ssem, rsem, dev):
        return pltpu.make_async_remote_copy(
            src_ref=src, dst_ref=dst, send_sem=ssem, recv_sem=rsem,
            device_id={"sp": dev}, device_id_type=pl.DeviceIdType.MESH)

    bar = pltpu.get_barrier_semaphore()
    for k in range(1, sp_n):
        pl.semaphore_signal(bar, inc=1, device_id={"sp": lax.rem(me + k, sp_n)}, device_id_type=pl.DeviceIdType.MESH)
    pl.semaphore_wait(bar, sp_n - 1)

    def img_copy(slot, g, dev):
        row = (3, 0, 1)[slot]
        part = pl.ds(g * GROUP, GROUP)
        return remote(img.at[part, row], halo.at[slot, part], im_send.at[slot, g], im_recv.at[slot, g], dev)

    @pl.loop(0, n_grp)
    def _(g):
        @pl.when(has_dn)
        def _():
            img_copy(0, g, dn).start()

        @pl.when(has_up)
        def _():
            img_copy(1, g, up).start()

    @pl.when(has_up)
    def _():
        @pl.loop(0, n_grp)
        def _(g):
            img_copy(2, g, up).start()

    @pl.when(jnp.logical_not(has_up))
    def _():
        @pl.loop(0, n_img)
        def _(n):
            halo[0, n] = jnp.zeros(halo.shape[2:], BF)
            hh[0, n] = jnp.zeros(hh.shape[2:], BF)
            rb[0, n] = jnp.zeros(rb.shape[2:], BF)

    @pl.when(jnp.logical_not(has_dn))
    def _():
        @pl.loop(0, n_img)
        def _(n):
            halo[1, n] = jnp.zeros(halo.shape[2:], BF)
            halo[2, n] = jnp.zeros(halo.shape[2:], BF)
            hh[1, n] = jnp.zeros(hh.shape[2:], BF)
            rb[1, n] = jnp.zeros(rb.shape[2:], BF)

    def dot(a, b):
        return jnp.dot(a, b, preferred_element_type=F32)

    def add_stats(carry, z):
        s, q = carry
        zz = z.reshape(z.shape[0] // 8, 8, z.shape[1])
        return s + jnp.sum(zz, axis=0), q + jnp.sum(zz * zz, axis=0)

    zero_stats = (jnp.zeros((8, 256), F32), jnp.zeros((8, 256), F32))

    def norm(z, m):
        return jnp.maximum((z - m[0]) * m[1] + m[2], 0.0)

    def moments(k, stats, count, fold64):
        s, q = (t[:, :128] + t[:, 128:] for t in stats)
        if fold64:
            s, q = s + pltpu.roll(s, 64, 1), q + pltpu.roll(q, 64, 1)
        own = cat([s, q], 0)
        msg[k] = own
        first = remote(msg.at[k], pslot.at[k], ar_send.at[k, 0], ar_recv.at[k, 3], me + 1 - 2 * core)
        first.start()
        first.wait_recv()
        mine = own + pslot[k]
        cmsg[k] = mine
        near = lax.rem(chip + 1 + core * (chips - 2), chips)
        far = lax.rem(chip + 2, chips)
        for c in range(2):
            remote(cmsg.at[k], slots.at[k, core], ar_send.at[k, 1 + c], ar_recv.at[k, core], near * 2 + c).start()

        @pl.when(core == OPP_CORE)
        def _():
            for c in range(2):
                remote(cmsg.at[k], slots.at[k, 2], ar_send.at[k, 3 + c], ar_recv.at[k, 2], far * 2 + c).start()

        for c in range(3):
            remote(cmsg.at[k], slots.at[k, c], ar_send.at[k, 1], ar_recv.at[k, c], me).wait_recv()
        tot = (mine + slots[k, 2]) + (slots[k, 0] + slots[k, 1])
        inv = 1.0 / count
        mean = jnp.sum(tot[:8], axis=0, keepdims=True) * inv
        var = jnp.sum(tot[8:], axis=0, keepdims=True) * inv - mean * mean
        p = bn[k]
        scale = p[0:1] * lax.rsqrt(var + NORM_EPS)
        return tuple(cat([t, t], 1) for t in (mean, scale, p[1:2]))

    def shifts(u):
        row = lax.rem(lax.broadcasted_iota(jnp.int32, (u.shape[0], 1), 0), half)
        zero = jnp.zeros_like(u)
        prev = jnp.where(row == 0, zero, pltpu.roll(u, 1, 0))
        nxt = jnp.where(row == half - 1, zero, pltpu.roll(u, u.shape[0] - 1, 0))
        return cat([prev, u, nxt], 1)

    def shifts_w(u):
        row = lax.broadcasted_iota(jnp.int32, (u.shape[0], 1), 0)
        zero = jnp.zeros_like(u)
        prev = jnp.where(row == 0, zero, pltpu.roll(u, 1, 0))
        nxt = jnp.where(row == u.shape[0] - 1, zero, pltpu.roll(u, u.shape[0] - 1, 0))
        return cat([prev, u, nxt], 1)

    def load(n):
        slot = lax.rem(n, SLOTS)
        return pltpu.make_async_copy(img.at[n], xb.at[slot], ld_sem.at[slot])

    for n in range(SLOTS - 1):
        load(n).start()

    def stage_a(g, carry):
        @pl.when(has_up)
        def _():
            img_copy(0, g, dn).wait_recv()

        @pl.when(has_dn)
        def _():
            img_copy(1, g, up).wait_recv()

        def one(i, carry):
            n = g * GROUP + i

            @pl.when(n + SLOTS - 1 < n_img)
            def _():
                load(n + SLOTS - 1).start()

            load(n).wait()
            x = xb.at[lax.rem(n, SLOTS)]
            t0 = cat([halo[0, n], x[0]], 0).T
            t1 = cat([x[1], x[2]], 0).T
            t2 = cat([x[3], halo[1, n]], 0).T
            xs[n] = t2
            z = dot(shifts_w(cat([t0, t1, t2], 1)), wa[...])
            za[0, n] = z[:, :128]
            za[1, n] = z[:, 128:]
            return add_stats(carry, z)

        return lax.fori_loop(0, GROUP, one, carry)

    m = moments(0, lax.fori_loop(0, n_grp, stage_a, zero_stats), count_a, True)
    m_half = tuple(t[:, :128] for t in m)

    def stage_d(g, carry):
        @pl.when(has_dn)
        def _():
            img_copy(2, g, up).wait_recv()

        def one(i, carry):
            n = g * GROUP + i
            t3 = cat([halo[2, n], halo[2, n]], 0).T
            z4[...] = dot(shifts_w(cat([xs[n], t3], 1)), w4[...])
            ev, od = pl.ds(0, half, stride=2), pl.ds(1, half, stride=2)
            e = norm(cat([za[0, n, ev, :], za[1, n, ev, :]], 1), m).astype(BF)
            o = norm(cat([za[0, n, od, :], za[1, n, od, :]], 1), m).astype(BF)
            e4 = jnp.where(has_dn, norm(z4[ev, :], m_half), 0.0).astype(BF)
            o4 = jnp.where(has_dn, norm(z4[od, :], m_half), 0.0).astype(BF)
            row = lax.broadcasted_iota(jnp.int32, (half, 1), 0)

            def nxt(t):
                return jnp.where(row == half - 1, jnp.zeros_like(t), pltpu.roll(t, half - 1, 0))

            z = dot(cat([e, o, nxt(e), e4, o4, nxt(e4)], 1), wd[...])
            zb[n] = z
            return add_stats(carry, z)

        return lax.fori_loop(0, GROUP, one, carry)

    m = moments(1, lax.fori_loop(0, n_grp, stage_d, zero_stats), count_b, False)

    def ex_copy(slot, g, src, dst, dev):
        part = pl.ds(g * GROUP, GROUP)
        return remote(src.at[1 - slot, part], dst.at[slot, part], ex_send.at[slot, g], ex_recv.at[slot, g], dev)

    def ex_start(g, src, dst):
        @pl.when(has_dn)
        def _():
            ex_copy(0, g, src, dst, dn).start()

        @pl.when(has_up)
        def _():
            ex_copy(1, g, src, dst, up).start()

    def ex_wait_send(src, dst):
        @pl.loop(0, n_grp)
        def _(g):
            @pl.when(has_dn)
            def _():
                ex_copy(0, g, src, dst, dn).wait_send()

            @pl.when(has_up)
            def _():
                ex_copy(1, g, src, dst, up).wait_send()

    def get(ref, part):
        return cat([ref[0, part].reshape(rows, 128), ref[1, part].reshape(rows, 128)], 1)

    def put(ref, part, v):
        ref[0, part] = v[:, :128].reshape(GROUP, half, 128)
        ref[1, part] = v[:, 128:].reshape(GROUP, half, 128)

    lane = lax.broadcasted_iota(jnp.int32, (1, 256), 1)
    valid = ((lane < 128) & has_up) | ((lane >= 128) & has_dn)

    for j in range(blocks):
        m_prev = m
        src, dst = (hb, hh) if j == 0 else (ub, rb)

        def conv_in(g, carry):
            part = pl.ds(g * GROUP, GROUP)
            z = zb[part].reshape(rows, 256)
            if j == 0:
                h = norm(z, m_prev).astype(BF)
            else:
                h = jnp.maximum((z - m_prev[0]) * m_prev[1] + m_prev[2] + get(hb, part).astype(F32), 0.0).astype(BF)
            put(hb, part, h)
            if j == 0:
                @pl.when(g > 0)
                def _():
                    ex_start(g - 1, src, dst)
            z = dot(h, w_in[j])
            zb[part] = z.reshape(GROUP, half, 256)
            return add_stats(carry, z)

        stats = lax.fori_loop(0, n_grp, conv_in, zero_stats)
        if j == 0:
            ex_start(n_grp - 1, src, dst)
        m_in = moments(2 + 3 * j, stats, count_b, False)

        def mid_local(g, carry):
            part = pl.ds(g * GROUP, GROUP)
            u = norm(zb[part].reshape(rows, 256), m_in).astype(BF)
            zb[part] = dot(shifts(u), w_loc[j]).reshape(GROUP, half, 256)
            return carry

        lax.fori_loop(0, n_grp, mid_local, 0)

        def mid_halo(g, carry):
            part = pl.ds(g * GROUP, GROUP)

            @pl.when(has_up)
            def _():
                ex_copy(0, g, src, dst, dn).wait_recv()

            @pl.when(has_dn)
            def _():
                ex_copy(1, g, src, dst, up).wait_recv()

            h = get(hh, part)
            if j > 0:
                z = dot(get(rb, part), w_out[j - 1])
                h = jnp.maximum((z - m_prev[0]) * m_prev[1] + m_prev[2] + h.astype(F32), 0.0).astype(BF)
                if j < blocks - 1:
                    put(hh, part, h)
            u = jnp.where(valid, norm(dot(h, w_in[j]), m_in), 0.0).astype(BF)
            z = zb[part].reshape(rows, 256) + dot(shifts(u), w_halo[j])
            zb[part] = z.reshape(GROUP, half, 256)
            return add_stats(carry, z)

        stats = lax.fori_loop(0, n_grp, mid_halo, zero_stats)
        ex_wait_send(src, dst)
        m_mid = moments(3 + 3 * j, stats, count_b, False)

        def conv_out(g, carry):
            part = pl.ds(g * GROUP, GROUP)
            u = norm(zb[part].reshape(rows, 256), m_mid).astype(BF)
            if j < blocks - 1:
                put(ub, part, u)

                @pl.when(g > 0)
                def _():
                    ex_start(g - 1, ub, rb)
            z = dot(u, w_out[j])
            zb[part] = z.reshape(GROUP, half, 256)
            return add_stats(carry, z)

        stats = lax.fori_loop(0, n_grp, conv_out, zero_stats)
        if j < blocks - 1:
            ex_start(n_grp - 1, ub, rb)
        m = moments(4 + 3 * j, stats, count_b, False)

    def out_copy(g, r):
        part = pl.ds(g * GROUP, GROUP)
        return pltpu.make_async_copy(hb.at[r, part], out.at[part, r], out_sem.at[r, g])

    def finish(g, carry):
        part = pl.ds(g * GROUP, GROUP)
        z = zb[part].reshape(rows, 256)
        h = jnp.maximum((z - m[0]) * m[1] + m[2] + get(hb, part).astype(F32), 0.0).astype(BF)
        put(hb, part, h)
        for r in range(2):
            out_copy(g, r).start()
        return carry

    lax.fori_loop(0, n_grp, finish, 0)

    @pl.loop(0, n_grp)
    def _(g):
        for r in range(2):
            out_copy(g, r).wait()

        @pl.when(has_dn)
        def _():
            img_copy(0, g, dn).wait_send()

        @pl.when(has_up)
        def _():
            img_copy(1, g, up).wait_send()
            img_copy(2, g, up).wait_send()

    @pl.loop(0, 2 + 3 * blocks)
    def _(k):
        remote(msg.at[k], pslot.at[k], ar_send.at[k, 0], ar_recv.at[k, 3], me).wait_send()
        for c in range(2):
            remote(cmsg.at[k], slots.at[k, 0], ar_send.at[k, 1 + c], ar_recv.at[k, 0], me).wait_send()

        @pl.when(core == OPP_CORE)
        def _():
            for c in range(2):
                remote(cmsg.at[k], slots.at[k, 2], ar_send.at[k, 3 + c], ar_recv.at[k, 2], me).wait_send()


def solution(mesh):
    sp_n = mesh.shape["sp"]

    def forward(images, w_a, bn_a, w_down, bn_down, w_in, bn_in, w_mid, bn_mid, w_out, bn_out):
        n_img, rows_dev, width, chan = images.shape
        half = width // 2
        blocks = w_in.shape[0]
        n_bn = 2 + 3 * blocks
        n_grp = n_img // GROUP
        packed = pack_weights(w_a, w_down, w_in, w_mid, w_out)
        rest = jnp.stack([bn_in, bn_mid, bn_out], axis=1).reshape(3 * blocks, 2, 128)
        bn = cat([jnp.tile(bn_a, (1, 1, 2)), bn_down[None], rest], 0)
        x = jnp.transpose(images, (0, 1, 3, 2))
        dims = (n_img, width, sp_n, blocks, n_img * rows_dev * width * sp_n, n_img * (rows_dev // 2) * half * sp_n)
        vmem = pl.BlockSpec(memory_space=pltpu.VMEM)
        anys = pl.BlockSpec(memory_space=pl.ANY)
        plane = (2, n_img, half, 128)
        return pl.pallas_call(
            functools.partial(body, dims),
            out_shape=jax.ShapeDtypeStruct((n_img, rows_dev // 2, half, 128), BF),
            in_specs=[anys] + [vmem] * 8,
            out_specs=anys,
            scratch_shapes=[
                pltpu.VMEM((SLOTS, rows_dev, chan, width), BF),
                pltpu.VMEM((3, n_img, chan, width), BF),
                pltpu.VMEM((n_img, width, 128), BF),
                pltpu.VMEM((2, n_img, width, 128), F32),
                pltpu.VMEM((width, 128), F32),
                pltpu.VMEM((n_img, half, 256), F32),
                pltpu.VMEM(plane, BF),
                pltpu.VMEM(plane, BF),
                pltpu.VMEM(plane, BF),
                pltpu.VMEM(plane, BF),
                pltpu.VMEM((n_bn, 16, 128), F32),
                pltpu.VMEM((n_bn, 16, 128), F32),
                pltpu.VMEM((n_bn, 16, 128), F32),
                pltpu.VMEM((n_bn, 3, 16, 128), F32),
                pltpu.SemaphoreType.DMA((SLOTS,)),
                pltpu.SemaphoreType.DMA((3, n_grp)),
                pltpu.SemaphoreType.DMA((3, n_grp)),
                pltpu.SemaphoreType.DMA((2, n_grp)),
                pltpu.SemaphoreType.DMA((2, n_grp)),
                pltpu.SemaphoreType.DMA((n_bn, 5)),
                pltpu.SemaphoreType.DMA((n_bn, 4)),
                pltpu.SemaphoreType.DMA((2, n_grp)),
            ],
            compiler_params=pltpu.CompilerParams(
                collective_id=0, has_side_effects=True, vmem_limit_bytes=67043328),
            name="stack",
        )(x, *packed, bn)

    act_spec = P("dp", "sp", None, None)
    return jax.shard_map(forward, mesh=mesh, in_specs=(act_spec,) + (P(),) * 10, out_specs=act_spec, check_vma=False)
```

time: 561 us -> 295 us (0.53); the launches traced: 550 us -> 295 us
  Pallas kernels: 0 us -> 250 us
  blocking collectives: 139 us -> 0 us
  matrix products: 126 us -> 0 us
  waiting for transfers between devices: 97.6 us -> 0 us
  other arithmetic: 89.1 us -> 16.3 us
  local copies, waits for them, and re-layouts: 73.4 us -> 27.7 us
  starting transfers between devices: 24.3 us -> 0 us
    pallas_call x0 -> x1, Pallas kernels: none -> 250 us  [forward(): pl.pallas_call(functools.partial(body, dims), out_shape=jax.ShapeDtypeStr...]
    psum x11 -> x0, blocking collectives: 139 us -> none  [batch_norm(): group_moments = lax.psum(part_sums, 'sp') / norm_count]
    ppermute x9 -> x0, waiting for transfers between devices: 97.6 us -> none  [the longest x4 60.9 us: conv_same(): from_above = lax.ppermute(hidden[:, -1:], 'sp', to_next)]
    convert_element_type x11 -> x0, other arithmetic: 88.8 us -> none  [the longest x8 59.8 us: norm_relu(): return jax.nn.relu(batch_norm(pre_act, params)).astype(jnp.bfloat16)]
    conv_general_dilated x5 -> x0, matrix products: 81.1 us -> none  [the longest x4 68 us: conv_same(): lax.conv_general_dilated(padded, weight, (1, 1), ((0, 0), (1, 1)), dimens...]
    dot_general x6 -> x0, matrix products: 45.2 us -> none  [conv_point(): jnp.einsum('bhwc,cd->bhwd', hidden, weight, preferred_element_type=jnp.fl...]
    ppermute x9 -> x0, starting transfers between devices: 24.3 us -> none  [the longest x4 10.4 us: conv_same(): from_above = lax.ppermute(hidden[:, -1:], 'sp', to_next)]
    ppermute x3 -> x0, local copies, waits for them, and re-layouts: 21.5 us -> none  [the longest x1 7.45 us: conv_same(): from_above = lax.ppermute(hidden[:, -1:], 'sp', to_next)]
  transfers between devices with their start and end apart: 9 -> 0, of which waited for: 7 -> 0; matrix products, arithmetic and copies ran while one was open for 6% -> 0% of each run, Pallas kernels for 0% -> 0%
where the time goes in v1:
time: 295 us
  Pallas kernels  250 us (85%)
  local copies, waits for them, and re-layouts  27.7 us (9%)
  other arithmetic  16.3 us (6%)
    pallas_call x1, Pallas kernels, forward(): pl.pallas_call(functools.partial(body, dims), out_shape=jax.ShapeDtypeStr...  250 us
    unnamed x35, local copies, waits for them, and re-layouts  23 us
    unnamed x30, other arithmetic  10.2 us

profile of v1, /device:TPU:81, one launch (start us, length us, event | category | flops | bytes accessed | tf_op | source)
XLA Modules:
  0.0 294.6 jit_solution(13213644339723533082)
XLA Ops:
  0.0 0.7 tile.12
  0.8 0.7 pad_maximum_fusion.17
  1.5 1.3 pad_maximum_fusion.16.bn
  2.8 0.8 slice_bitcast_fusion.32
  3.6 0.8 slice_bitcast_fusion.29
  4.5 0.9 slice_bitcast_fusion.42
  12.6 0.8 pad_maximum_fusion.3.w_out
  13.4 0.8 pad_maximum_fusion.2.w_in
  14.9 0.6 constant_dynamic-update-slice_fusion.46
  17.3 0.6 constant_dynamic-update-slice_fusion.42
  19.7 0.6 constant_dynamic-update-slice_fusion.38
  22.2 0.6 constant_dynamic-update-slice_fusion.34
  23.4 0.6 constant_dynamic-update-slice_fusion.32
  25.2 0.7 constant_dynamic-update-slice_fusion.16
  25.9 0.7 constant_dynamic-update-slice_fusion.15
  26.6 0.7 constant_dynamic-update-slice_fusion.14
  27.3 0.7 constant_dynamic-update-slice_fusion.13
  28.0 0.7 constant_dynamic-update-slice_fusion.12
  29.2 0.7 constant_dynamic-update-slice_fusion.10
  29.9 0.7 constant_dynamic-update-slice_fusion.9
  30.6 0.7 constant_dynamic-update-slice_fusion.8
  31.3 0.7 constant_dynamic-update-slice_fusion.7
  32.0 0.7 constant_dynamic-update-slice_fusion.6
  33.3 0.7 constant_dynamic-update-slice_fusion.4
  34.0 0.7 constant_dynamic-update-slice_fusion.3
  34.6 0.7 constant_dynamic-update-slice_fusion.2
  35.3 0.7 constant_dynamic-update-slice_fusion.1
  36.0 0.7 constant_dynamic-update-slice_fusion
  37.1 1.2 pad_maximum_fusion.1.w_halo
  38.3 1.1 pad_maximum_fusion.w_loc
  39.5 250.4 %stack.81 = bf16[32,2,256,128]{3,2,1,0:T(8,128)(2,1)} custom-call(bf16[32,4,64,512]{3,2,1,0:T(8,128)(2,1)} %bitcast.127, bf16[1152,256]{1,0:T(8,128)(2,1)} %get-tuple-element.98.wa, bf16[768,128]{1,0:T(8,128)(2,1)} %constant_dynamic-update-slice_fusion.18.w4, bf16[1152,256]{1,0:T(8,128)(2,1)} %get-tuple-element.99.wd, ...), custom_call_target="tpu_custom_call" | custom-call | tf_op jit(solution)/shard_map/stack/pallas_call | solution.py:426
  289.9 4.7 %copy.89 = bf16[32,2,256,128]{3,2,1,0:T(8,128)(2,1)} copy(bf16[32,2,256,128]{3,2,1,0:T(8,128)(2,1)} %stack.81) | data formatting | bytes 8388608
  (59 shorter events, 16.8 us)
Async XLA Ops:
  0.0 5.3 %copy-start.1 = (bf16[3,3,64,128]{3,2,1,0:T(8,128)(2,1)S(1)}, bf16[3,3,64,128]{3,2,1,0:T(8,128)(2,1)}, u32[]{:S(2)}) copy-start(bf16[3,3,64,128]{3,2,1,0:T(8,128)(2,1)} %param.14) | copy-start | bytes 442372
  9.6 4.7 %copy-start = (bf16[3,3,3,128,128]{4,3,2,1,0:T(8,128)(2,1)S(1)}, bf16[3,3,3,128,128]{4,3,2,1,0:T(8,128)(2,1)}, u32[]{:S(2)}) copy-start(bf16[3,3,3,128,128]{4,3,2,1,0:T(8,128)(2,1)} %param.18) | copy-start | bytes 2654212

commit v2 on v1

--- a/solution.py
+++ b/solution.py
@@ -31,43 +31,37 @@
     return cat(rows, 0)
 
 
-def pack_weights(w_a, w_down, w_in, w_mid, w_out):
-    blocks = w_in.shape[0]
-    wa, w4, wdn, wdh = [], [], [], []
+def pack_stage_a(w_a, w_down, wa, w4, wd):
     for dx in range(3):
         ta = [w_a[0, dy, dx] for dy in range(3)]
         zero = jnp.zeros_like(ta[0])
-        wa.append(banded(ta, range(6), range(4), 1, 0))
-        w4.append(cat([cat([t, zero], 1) for t in ta + [zero]], 0))
+        wa[pl.ds(dx * 384, 384)] = banded(ta, range(6), range(4), 1, 0)
+        w4[pl.ds(dx * 256, 256)] = cat([cat([t, zero], 1) for t in ta + [zero]], 0)
         td = [w_down[dy, dx] for dy in range(3)]
-        wdn.append(banded(td, range(4), range(2), 2, 0))
-        wdh.append(banded(td + [jnp.zeros_like(td[0])], (4, 5), (0, 1), 2, 0))
-    wa, w4, wd = cat(wa, 0), cat(w4, 0), cat(wdn + wdh, 0)
-
-    def diag(w):
-        z = jnp.zeros_like(w)
-        return cat([cat([w, z], 1), cat([z, w], 1)], 0)
-
-    w_in2 = jnp.stack([diag(w_in[j]) for j in range(blocks)])
-    w_out2 = jnp.stack([diag(w_out[j]) for j in range(blocks)])
-    loc, halo = [], []
-    for j in range(blocks):
-        ml, mh = [], []
+        wd[pl.ds(dx * 256, 256)] = banded(td, range(4), range(2), 2, 0)
+        wd[pl.ds(768 + dx * 128, 128)] = banded(td + [jnp.zeros_like(td[0])], (4, 5), (0, 1), 2, 0)
+
+
+def pack_stage_b(w_in, w_mid, w_out, in2, out2, loc, halo):
+    def diag(a, b):
+        z = jnp.zeros_like(a)
+        return cat([cat([a, z], 1), cat([z, b], 1)], 0)
+
+    for j in range(w_in.shape[0]):
+        in2[j] = diag(w_in[j], w_in[j])
+        out2[j] = diag(w_out[j], w_out[j])
         for dx in range(3):
             tm = [w_mid[j, dy, dx] for dy in range(3)]
-            z = jnp.zeros_like(tm[0])
-            ml.append(banded(tm, (0, 1), (0, 1), 1, 1))
-            mh.append(cat([cat([tm[0], z], 1), cat([z, tm[2]], 1)], 0))
-        loc.append(cat(ml, 0))
-        halo.append(cat(mh, 0))
-    return wa, w4, wd, w_in2, w_out2, jnp.stack(loc), jnp.stack(halo)
+            loc[j, pl.ds(dx * 256, 256)] = banded(tm, (0, 1), (0, 1), 1, 1)
+            halo[j, pl.ds(dx * 256, 256)] = diag(tm[0], tm[2])
 
 
 def body(
-    dims, img, wa, w4, wd, w_in, w_out, w_loc, w_halo, bn, out,
+    dims, img, w_a_hbm, w_down_hbm, w_in_hbm, w_mid_hbm, w_out_hbm, bn_a, bn_down, bn_in, bn_mid, bn_out, out,
+    w_a_raw, w_down_raw, w_in_raw, w_mid_raw, w_out_raw, wa, w4, wd, w_in, w_out, w_loc, w_halo,
     xb, halo, xs, za, z4, zb, hb, ub, hh, rb,
     msg, pslot, cmsg, slots,
-    ld_sem, im_send, im_recv, ex_send, ex_recv, ar_send, ar_recv, out_sem,
+    ld_sem, im_send, im_recv, ex_send, ex_recv, ar_send, ar_recv, out_sem, w_sem,
 ):
     n_img, width, sp_n, blocks, count_a, count_b = dims
     half = width // 2
@@ -87,6 +81,19 @@
             src_ref=src, dst_ref=dst, send_sem=ssem, recv_sem=rsem,
             device_id={"sp": dev}, device_id_type=pl.DeviceIdType.MESH)
 
+    w_copies = [
+        pltpu.make_async_copy(src, dst, w_sem.at[i]) for i, (src, dst) in enumerate((
+            (w_a_hbm, w_a_raw), (w_down_hbm, w_down_raw), (w_in_hbm, w_in_raw), (w_mid_hbm, w_mid_raw), (w_out_hbm, w_out_raw)))]
+    for copy in w_copies:
+        copy.start()
+
+    def load(n):
+        slot = lax.rem(n, SLOTS)
+        return pltpu.make_async_copy(img.at[n], xb.at[slot], ld_sem.at[slot])
+
+    for n in range(SLOTS - 1):
+        load(n).start()
+
     bar = pltpu.get_barrier_semaphore()
     for k in range(1, sp_n):
         pl.semaphore_signal(bar, inc=1, device_id={"sp": lax.rem(me + k, sp_n)}, device_id_type=pl.DeviceIdType.MESH)
@@ -143,7 +150,7 @@
     def norm(z, m):
         return jnp.maximum((z - m[0]) * m[1] + m[2], 0.0)
 
-    def moments(k, stats, count, fold64):
+    def moments(k, stats, count, p, fold64=False):
         s, q = (t[:, :128] + t[:, 128:] for t in stats)
         if fold64:
             s, q = s + pltpu.roll(s, 64, 1), q + pltpu.roll(q, 64, 1)
@@ -170,7 +177,6 @@
         inv = 1.0 / count
         mean = jnp.sum(tot[:8], axis=0, keepdims=True) * inv
         var = jnp.sum(tot[8:], axis=0, keepdims=True) * inv - mean * mean
-        p = bn[k]
         scale = p[0:1] * lax.rsqrt(var + NORM_EPS)
         return tuple(cat([t, t], 1) for t in (mean, scale, p[1:2]))
 
@@ -188,12 +194,10 @@
         nxt = jnp.where(row == u.shape[0] - 1, zero, pltpu.roll(u, u.shape[0] - 1, 0))
         return cat([prev, u, nxt], 1)
 
-    def load(n):
-        slot = lax.rem(n, SLOTS)
-        return pltpu.make_async_copy(img.at[n], xb.at[slot], ld_sem.at[slot])
-
-    for n in range(SLOTS - 1):
-        load(n).start()
+    for copy in w_copies:
+        copy.wait()
+    pack_stage_a(w_a_raw, w_down_raw, wa, w4, wd)
+    pack_stage_b(w_in_raw, w_mid_raw, w_out_raw, w_in, w_out, w_loc, w_halo)
 
     def stage_a(g, carry):
         @pl.when(has_up)
@@ -224,7 +228,7 @@
 
         return lax.fori_loop(0, GROUP, one, carry)
 
-    m = moments(0, lax.fori_loop(0, n_grp, stage_a, zero_stats), count_a, True)
+    m = moments(0, lax.fori_loop(0, n_grp, stage_a, zero_stats), count_a, cat([bn_a[0], bn_a[0]], 1), True)
     m_half = tuple(t[:, :128] for t in m)
 
     def stage_d(g, carry):
@@ -252,7 +256,7 @@
 
         return lax.fori_loop(0, GROUP, one, carry)
 
-    m = moments(1, lax.fori_loop(0, n_grp, stage_d, zero_stats), count_b, False)
+    m = moments(1, lax.fori_loop(0, n_grp, stage_d, zero_stats), count_b, bn_down[...])
 
     def ex_copy(slot, g, src, dst, dev):
         part = pl.ds(g * GROUP, GROUP)
@@ -311,7 +315,7 @@
         stats = lax.fori_loop(0, n_grp, conv_in, zero_stats)
         if j == 0:
             ex_start(n_grp - 1, src, dst)
-        m_in = moments(2 + 3 * j, stats, count_b, False)
+        m_in = moments(2 + 3 * j, stats, count_b, bn_in[j])
 
         def mid_local(g, carry):
             part = pl.ds(g * GROUP, GROUP)
@@ -345,7 +349,7 @@
 
         stats = lax.fori_loop(0, n_grp, mid_halo, zero_stats)
         ex_wait_send(src, dst)
-        m_mid = moments(3 + 3 * j, stats, count_b, False)
+        m_mid = moments(3 + 3 * j, stats, count_b, bn_mid[j])
 
         def conv_out(g, carry):
             part = pl.ds(g * GROUP, GROUP)
@@ -363,7 +367,7 @@
         stats = lax.fori_loop(0, n_grp, conv_out, zero_stats)
         if j < blocks - 1:
             ex_start(n_grp - 1, ub, rb)
-        m = moments(4 + 3 * j, stats, count_b, False)
+        m = moments(4 + 3 * j, stats, count_b, bn_out[j])
 
     def out_copy(g, r):
         part = pl.ds(g * GROUP, GROUP)
@@ -415,9 +419,6 @@
         blocks = w_in.shape[0]
         n_bn = 2 + 3 * blocks
         n_grp = n_img // GROUP
-        packed = pack_weights(w_a, w_down, w_in, w_mid, w_out)
-        rest = jnp.stack([bn_in, bn_mid, bn_out], axis=1).reshape(3 * blocks, 2, 128)
-        bn = cat([jnp.tile(bn_a, (1, 1, 2)), bn_down[None], rest], 0)
         x = jnp.transpose(images, (0, 1, 3, 2))
         dims = (n_img, width, sp_n, blocks, n_img * rows_dev * width * sp_n, n_img * (rows_dev // 2) * half * sp_n)
         vmem = pl.BlockSpec(memory_space=pltpu.VMEM)
@@ -426,9 +427,21 @@
         return pl.pallas_call(
             functools.partial(body, dims),
             out_shape=jax.ShapeDtypeStruct((n_img, rows_dev // 2, half, 128), BF),
-            in_specs=[anys] + [vmem] * 8,
+            in_specs=[anys] * 6 + [vmem] * 5,
             out_specs=anys,
             scratch_shapes=[
+                pltpu.VMEM(w_a.shape, BF),
+                pltpu.VMEM(w_down.shape, BF),
+                pltpu.VMEM(w_in.shape, BF),
+                pltpu.VMEM(w_mid.shape, BF),
+                pltpu.VMEM(w_out.shape, BF),
+                pltpu.VMEM((1152, 256), BF),
+                pltpu.VMEM((768, 128), BF),
+                pltpu.VMEM((1152, 256), BF),
+                pltpu.VMEM((blocks, 256, 256), BF),
+                pltpu.VMEM((blocks, 256, 256), BF),
+                pltpu.VMEM((blocks, 768, 256), BF),
+                pltpu.VMEM((blocks, 768, 256), BF),
                 pltpu.VMEM((SLOTS, rows_dev, chan, width), BF),
                 pltpu.VMEM((3, n_img, chan, width), BF),
                 pltpu.VMEM((n_img, width, 128), BF),
@@ -451,11 +464,12 @@
                 pltpu.SemaphoreType.DMA((n_bn, 5)),
                 pltpu.SemaphoreType.DMA((n_bn, 4)),
                 pltpu.SemaphoreType.DMA((2, n_grp)),
+                pltpu.SemaphoreType.DMA((5,)),
             ],
             compiler_params=pltpu.CompilerParams(
                 collective_id=0, has_side_effects=True, vmem_limit_bytes=67043328),
             name="stack",
-        )(x, *packed, bn)
+        )(x, w_a, w_down, w_in, w_mid, w_out, bn_a, bn_down, bn_in, bn_mid, bn_out)
 
     act_spec = P("dp", "sp", None, None)
     return jax.shard_map(forward, mesh=mesh, in_specs=(act_spec,) + (P(),) * 10, out_specs=act_spec, check_vma=False)

time: 295 us -> 254 us (0.86)
  local copies, waits for them, and re-layouts: 27.7 us -> 4.7 us
  other arithmetic: 16.3 us -> 0 us
    unnamed x35 -> x1, local copies, waits for them, and re-layouts: 23 us -> 4.7 us
    unnamed x30 -> x0, other arithmetic: 10.2 us -> none
    another operation x9 -> x0, other arithmetic: 4.74 us -> none  [the longest x2 2.35 us: pack_weights(): return (wa, w4, wd, w_in2, w_out2, jnp.stack(loc), jnp.stack(halo))]
where the time goes in v2:
time: 254 us
  Pallas kernels  249 us (98%)
  local copies, waits for them, and re-layouts  4.7 us (2%)
    pallas_call x1, Pallas kernels, forward(): pl.pallas_call(functools.partial(body, dims), out_shape=jax.ShapeDtypeStr...  249 us

profile of v2, /device:TPU:81, one launch (start us, length us, event | category | flops | bytes accessed | tf_op | source)
XLA Modules:
  0.0 253.6 jit_solution(3721710139605557909)
XLA Ops:
  0.0 248.9 %stack.1 = bf16[32,2,256,128]{3,2,1,0:T(8,128)(2,1)} custom-call(bf16[32,4,64,512]{3,2,1,0:T(8,128)(2,1)} %bitcast.1, bf16[1,3,3,64,64]{4,3,2,1,0:T(8,128)(2,1)} %w_a_hbm.1, bf16[3,3,64,128]{3,2,1,0:T(8,128)(2,1)} %w_down_hbm.1, bf16[3,128,128]{2,1,0:T(8,128)(2,1)} %w_in_hbm.1, bf16[3,3,3,128,128]{4,3,2,1,0:T(8,128)(2,1)} %w_mid_hbm.1, ...), custom_call_target="tpu_custom_call" | custom-call | tf_op jit(solution)/shard_map/stack/pallas_call | solution.py:427
  248.9 4.7 %copy.13 = bf16[32,2,256,128]{3,2,1,0:T(8,128)(2,1)} copy(bf16[32,2,256,128]{3,2,1,0:T(8,128)(2,1)} %stack.1) | data formatting | bytes 8388608

commit v3 on v2

--- a/solution.py
+++ b/solution.py
@@ -10,9 +10,7 @@
 NORM_EPS = 1e-5
 BF = jnp.bfloat16
 F32 = jnp.float32
-OPP_CORE = 0
 GROUP = 4
-SLOTS = 4
 
 
 def cat(parts, axis):
@@ -36,13 +34,15 @@
         ta = [w_a[0, dy, dx] for dy in range(3)]
         zero = jnp.zeros_like(ta[0])
         wa[pl.ds(dx * 384, 384)] = banded(ta, range(6), range(4), 1, 0)
-        w4[pl.ds(dx * 256, 256)] = cat([cat([t, zero], 1) for t in ta + [zero]], 0)
+        w4[pl.ds(dx * 256, 256)] = cat([cat([t, t], 1) for t in ta + [zero]], 0)
         td = [w_down[dy, dx] for dy in range(3)]
         wd[pl.ds(dx * 256, 256)] = banded(td, range(4), range(2), 2, 0)
-        wd[pl.ds(768 + dx * 128, 128)] = banded(td + [jnp.zeros_like(td[0])], (4, 5), (0, 1), 2, 0)
-
-
-def pack_stage_b(w_in, w_mid, w_out, in2, out2, loc, halo):
+        none = jnp.zeros_like(td[2])
+        wd[pl.ds(768 + dx * 64, 64)] = cat([none, td[2]], 1)
+    wd[pl.ds(960, 64)] = jnp.zeros((64, 256), BF)
+
+
+def pack_stage_b(w_in, w_mid, w_out, in2, out2, mid2):
     def diag(a, b):
         z = jnp.zeros_like(a)
         return cat([cat([a, z], 1), cat([z, b], 1)], 0)
@@ -52,14 +52,14 @@
         out2[j] = diag(w_out[j], w_out[j])
         for dx in range(3):
             tm = [w_mid[j, dy, dx] for dy in range(3)]
-            loc[j, pl.ds(dx * 256, 256)] = banded(tm, (0, 1), (0, 1), 1, 1)
-            halo[j, pl.ds(dx * 256, 256)] = diag(tm[0], tm[2])
+            mid2[j, pl.ds(dx * 256, 256)] = banded(tm, (0, 1), (0, 1), 1, 1)
+            mid2[j, pl.ds(768 + dx * 256, 256)] = diag(tm[0], tm[2])
 
 
 def body(
     dims, img, w_a_hbm, w_down_hbm, w_in_hbm, w_mid_hbm, w_out_hbm, bn_a, bn_down, bn_in, bn_mid, bn_out, out,
-    w_a_raw, w_down_raw, w_in_raw, w_mid_raw, w_out_raw, wa, w4, wd, w_in, w_out, w_loc, w_halo,
-    xb, halo, xs, za, z4, zb, hb, ub, hh, rb,
+    w_a_raw, w_down_raw, w_in_raw, w_mid_raw, w_out_raw, wa, w4, wd, w_in, w_out, w_mid,
+    xb, halo, za, z4, zb, hb, ub, hh, rb,
     msg, pslot, cmsg, slots,
     ld_sem, im_send, im_recv, ex_send, ex_recv, ar_send, ar_recv, out_sem, w_sem,
 ):
@@ -67,6 +67,7 @@
     half = width // 2
     n_grp = n_img // GROUP
     rows = GROUP * half
+    fold = rows // width
     me = lax.axis_index("sp")
     core = lax.rem(me, 2)
     chip = lax.div(me, 2)
@@ -87,12 +88,11 @@
     for copy in w_copies:
         copy.start()
 
-    def load(n):
-        slot = lax.rem(n, SLOTS)
-        return pltpu.make_async_copy(img.at[n], xb.at[slot], ld_sem.at[slot])
-
-    for n in range(SLOTS - 1):
-        load(n).start()
+    def load(g):
+        slot = lax.rem(g, 2)
+        return pltpu.make_async_copy(img.at[pl.ds(g * GROUP, GROUP)], xb.at[slot], ld_sem.at[slot])
+
+    load(0).start()
 
     bar = pltpu.get_barrier_semaphore()
     for k in range(1, sp_n):
@@ -150,7 +150,7 @@
     def norm(z, m):
         return jnp.maximum((z - m[0]) * m[1] + m[2], 0.0)
 
-    def moments(k, stats, count, p, fold64=False):
+    def moments(k, stats, count, p, fold64=False, meanwhile=None):
         s, q = (t[:, :128] + t[:, 128:] for t in stats)
         if fold64:
             s, q = s + pltpu.roll(s, 64, 1), q + pltpu.roll(q, 64, 1)
@@ -166,11 +166,13 @@
         for c in range(2):
             remote(cmsg.at[k], slots.at[k, core], ar_send.at[k, 1 + c], ar_recv.at[k, core], near * 2 + c).start()
 
-        @pl.when(core == OPP_CORE)
+        @pl.when(core == lax.rem(chip, 2))
         def _():
             for c in range(2):
                 remote(cmsg.at[k], slots.at[k, 2], ar_send.at[k, 3 + c], ar_recv.at[k, 2], far * 2 + c).start()
 
+        if meanwhile is not None:
+            meanwhile()
         for c in range(3):
             remote(cmsg.at[k], slots.at[k, c], ar_send.at[k, 1], ar_recv.at[k, c], me).wait_recv()
         tot = (mine + slots[k, 2]) + (slots[k, 0] + slots[k, 1])
@@ -180,26 +182,23 @@
         scale = p[0:1] * lax.rsqrt(var + NORM_EPS)
         return tuple(cat([t, t], 1) for t in (mean, scale, p[1:2]))
 
-    def shifts(u):
-        row = lax.rem(lax.broadcasted_iota(jnp.int32, (u.shape[0], 1), 0), half)
+    def shifts(u, line):
+        row = lax.rem(lax.broadcasted_iota(jnp.int32, (u.shape[0], 1), 0), line)
         zero = jnp.zeros_like(u)
         prev = jnp.where(row == 0, zero, pltpu.roll(u, 1, 0))
-        nxt = jnp.where(row == half - 1, zero, pltpu.roll(u, u.shape[0] - 1, 0))
-        return cat([prev, u, nxt], 1)
-
-    def shifts_w(u):
-        row = lax.broadcasted_iota(jnp.int32, (u.shape[0], 1), 0)
-        zero = jnp.zeros_like(u)
-        prev = jnp.where(row == 0, zero, pltpu.roll(u, 1, 0))
-        nxt = jnp.where(row == u.shape[0] - 1, zero, pltpu.roll(u, u.shape[0] - 1, 0))
+        nxt = jnp.where(row == line - 1, zero, pltpu.roll(u, u.shape[0] - 1, 0))
         return cat([prev, u, nxt], 1)
 
     for copy in w_copies:
         copy.wait()
     pack_stage_a(w_a_raw, w_down_raw, wa, w4, wd)
-    pack_stage_b(w_in_raw, w_mid_raw, w_out_raw, w_in, w_out, w_loc, w_halo)
+    pack_stage_b(w_in_raw, w_mid_raw, w_out_raw, w_in, w_out, w_mid)
 
     def stage_a(g, carry):
+        @pl.when(g + 1 < n_grp)
+        def _():
+            load(g + 1).start()
+
         @pl.when(has_up)
         def _():
             img_copy(0, g, dn).wait_recv()
@@ -208,53 +207,51 @@
         def _():
             img_copy(1, g, up).wait_recv()
 
-        def one(i, carry):
+        load(g).wait()
+        for i in range(GROUP):
             n = g * GROUP + i
-
-            @pl.when(n + SLOTS - 1 < n_img)
-            def _():
-                load(n + SLOTS - 1).start()
-
-            load(n).wait()
-            x = xb.at[lax.rem(n, SLOTS)]
+            x = xb.at[lax.rem(g, 2), i]
             t0 = cat([halo[0, n], x[0]], 0).T
             t1 = cat([x[1], x[2]], 0).T
             t2 = cat([x[3], halo[1, n]], 0).T
-            xs[n] = t2
-            z = dot(shifts_w(cat([t0, t1, t2], 1)), wa[...])
+            hb[0, n] = t2[:half]
+            hb[1, n] = t2[half:]
+            z = dot(shifts(cat([t0, t1, t2], 1), width), wa[...])
             za[0, n] = z[:, :128]
             za[1, n] = z[:, 128:]
-            return add_stats(carry, z)
-
-        return lax.fori_loop(0, GROUP, one, carry)
+            carry = add_stats(carry, z)
+        return carry
 
     m = moments(0, lax.fori_loop(0, n_grp, stage_a, zero_stats), count_a, cat([bn_a[0], bn_a[0]], 1), True)
     m_half = tuple(t[:, :128] for t in m)
 
+    low = lax.broadcasted_iota(jnp.int32, (1, 128), 1) < 64
+
     def stage_d(g, carry):
         @pl.when(has_dn)
         def _():
             img_copy(2, g, up).wait_recv()
 
-        def one(i, carry):
+        for i in range(GROUP):
             n = g * GROUP + i
+            t2 = cat([hb[0, n], hb[1, n]], 0)
             t3 = cat([halo[2, n], halo[2, n]], 0).T
-            z4[...] = dot(shifts_w(cat([xs[n], t3], 1)), w4[...])
+            z4[i] = dot(shifts(cat([t2, t3], 1), width), w4[...])
+        for i in range(GROUP):
+            n = g * GROUP + i
             ev, od = pl.ds(0, half, stride=2), pl.ds(1, half, stride=2)
             e = norm(cat([za[0, n, ev, :], za[1, n, ev, :]], 1), m).astype(BF)
             o = norm(cat([za[0, n, od, :], za[1, n, od, :]], 1), m).astype(BF)
-            e4 = jnp.where(has_dn, norm(z4[ev, :], m_half), 0.0).astype(BF)
-            o4 = jnp.where(has_dn, norm(z4[od, :], m_half), 0.0).astype(BF)
+            b4 = jnp.where(has_dn, norm(jnp.where(low, z4[i, ev, :], z4[i, od, :]), m_half), 0.0).astype(BF)
             row = lax.broadcasted_iota(jnp.int32, (half, 1), 0)
 
             def nxt(t):
                 return jnp.where(row == half - 1, jnp.zeros_like(t), pltpu.roll(t, half - 1, 0))
 
-            z = dot(cat([e, o, nxt(e), e4, o4, nxt(e4)], 1), wd[...])
+            z = dot(cat([e, o, nxt(e), b4, nxt(b4)], 1), wd[...])
             zb[n] = z
-            return add_stats(carry, z)
-
-        return lax.fori_loop(0, GROUP, one, carry)
+            carry = add_stats(carry, z)
+        return carry
 
     m = moments(1, lax.fori_loop(0, n_grp, stage_d, zero_stats), count_b, bn_down[...])
 
@@ -315,17 +312,7 @@
         stats = lax.fori_loop(0, n_grp, conv_in, zero_stats)
         if j == 0:
             ex_start(n_grp - 1, src, dst)
-        m_in = moments(2 + 3 * j, stats, count_b, bn_in[j])
-
-        def mid_local(g, carry):
-            part = pl.ds(g * GROUP, GROUP)
-            u = norm(zb[part].reshape(rows, 256), m_in).astype(BF)
-            zb[part] = dot(shifts(u), w_loc[j]).reshape(GROUP, half, 256)
-            return carry
-
-        lax.fori_loop(0, n_grp, mid_local, 0)
-
-        def mid_halo(g, carry):
+        def prep(g, slot):
             part = pl.ds(g * GROUP, GROUP)
 
             @pl.when(has_up)
@@ -342,12 +329,30 @@
                 h = jnp.maximum((z - m_prev[0]) * m_prev[1] + m_prev[2] + h.astype(F32), 0.0).astype(BF)
                 if j < blocks - 1:
                     put(hh, part, h)
-            u = jnp.where(valid, norm(dot(h, w_in[j]), m_in), 0.0).astype(BF)
-            z = zb[part].reshape(rows, 256) + dot(shifts(u), w_halo[j])
+            z = dot(h, w_in[j])
+            for c in range(2):
+                za[c, pl.ds(slot * fold, fold)] = z[:, c * 128:(c + 1) * 128].reshape(fold, width, 128)
+
+        def main(g, slot, carry):
+            part = pl.ds(g * GROUP, GROUP)
+            zh = cat([za[c, pl.ds(slot * fold, fold)].reshape(rows, 128) for c in range(2)], 1)
+            u = norm(zb[part].reshape(rows, 256), m_in).astype(BF)
+            v = jnp.where(valid, norm(zh, m_in), 0.0).astype(BF)
+            z = dot(cat([shifts(u, half), shifts(v, half)], 1), w_mid[j])
             zb[part] = z.reshape(GROUP, half, 256)
             return add_stats(carry, z)
 
-        stats = lax.fori_loop(0, n_grp, mid_halo, zero_stats)
+        m_in = moments(2 + 3 * j, stats, count_b, bn_in[j], meanwhile=lambda: prep(0, 0))
+
+        def conv_mid(i, carry):
+            prep(2 * i + 1, 1)
+            carry = main(2 * i, 0, carry)
+            prep(2 * i + 2, 0)
+            return main(2 * i + 1, 1, carry)
+
+        stats = lax.fori_loop(0, n_grp // 2 - 1, conv_mid, zero_stats)
+        prep(n_grp - 1, 1)
+        stats = main(n_grp - 1, 1, main(n_grp - 2, 0, stats))
         ex_wait_send(src, dst)
         m_mid = moments(3 + 3 * j, stats, count_b, bn_mid[j])
 
@@ -404,7 +409,7 @@
         for c in range(2):
             remote(cmsg.at[k], slots.at[k, 0], ar_send.at[k, 1 + c], ar_recv.at[k, 0], me).wait_send()
 
-        @pl.when(core == OPP_CORE)
+        @pl.when(core == lax.rem(chip, 2))
         def _():
             for c in range(2):
                 remote(cmsg.at[k], slots.at[k, 2], ar_send.at[k, 3 + c], ar_recv.at[k, 2], me).wait_send()
@@ -437,16 +442,14 @@
                 pltpu.VMEM(w_out.shape, BF),
                 pltpu.VMEM((1152, 256), BF),
                 pltpu.VMEM((768, 128), BF),
-                pltpu.VMEM((1152, 256), BF),
+                pltpu.VMEM((1024, 256), BF),
                 pltpu.VMEM((blocks, 256, 256), BF),
                 pltpu.VMEM((blocks, 256, 256), BF),
-                pltpu.VMEM((blocks, 768, 256), BF),
-                pltpu.VMEM((blocks, 768, 256), BF),
-                pltpu.VMEM((SLOTS, rows_dev, chan, width), BF),
+                pltpu.VMEM((blocks, 1536, 256), BF),
+                pltpu.VMEM((2, GROUP, rows_dev, chan, width), BF),
                 pltpu.VMEM((3, n_img, chan, width), BF),
-                pltpu.VMEM((n_img, width, 128), BF),
                 pltpu.VMEM((2, n_img, width, 128), F32),
-                pltpu.VMEM((width, 128), F32),
+                pltpu.VMEM((GROUP, width, 128), F32),
                 pltpu.VMEM((n_img, half, 256), F32),
                 pltpu.VMEM(plane, BF),
                 pltpu.VMEM(plane, BF),
@@ -456,7 +459,7 @@
                 pltpu.VMEM((n_bn, 16, 128), F32),
                 pltpu.VMEM((n_bn, 16, 128), F32),
                 pltpu.VMEM((n_bn, 3, 16, 128), F32),
-                pltpu.SemaphoreType.DMA((SLOTS,)),
+                pltpu.SemaphoreType.DMA((2,)),
                 pltpu.SemaphoreType.DMA((3, n_grp)),
                 pltpu.SemaphoreType.DMA((3, n_grp)),
                 pltpu.SemaphoreType.DMA((2, n_grp)),

time: 254 us -> 183 us (0.72)
  Pallas kernels: 249 us -> 178 us
    pallas_call x1, Pallas kernels: 249 us -> 178 us  [forward(): pl.pallas_call(functools.partial(body, dims), out_shape=jax.ShapeDtypeStr...]
where the time goes in v3:
time: 183 us
  Pallas kernels  178 us (97%)
  local copies, waits for them, and re-layouts  4.7 us (3%)
    pallas_call x1, Pallas kernels, forward(): pl.pallas_call(functools.partial(body, dims), out_shape=jax.ShapeDtypeStr...  178 us
    unnamed x1, local copies, waits for them, and re-layouts  4.7 us

profile of v3, /device:TPU:81, one launch (start us, length us, event | category | flops | bytes accessed | tf_op | source)
XLA Modules:
  0.0 183.1 jit_solution(4645974956512784964)
XLA Ops:
  0.0 178.4 %stack.1 = bf16[32,2,256,128]{3,2,1,0:T(8,128)(2,1)} custom-call(bf16[32,4,64,512]{3,2,1,0:T(8,128)(2,1)} %bitcast.1, bf16[1,3,3,64,64]{4,3,2,1,0:T(8,128)(2,1)} %w_a_hbm.1, bf16[3,3,64,128]{3,2,1,0:T(8,128)(2,1)} %w_down_hbm.1, bf16[3,128,128]{2,1,0:T(8,128)(2,1)} %w_in_hbm.1, bf16[3,3,3,128,128]{4,3,2,1,0:T(8,128)(2,1)} %w_mid_hbm.1, ...), custom_call_target="tpu_custom_call" | custom-call | tf_op jit(solution)/shard_map/stack/pallas_call | solution.py:432
  178.4 4.7 %copy.13 = bf16[32,2,256,128]{3,2,1,0:T(8,128)(2,1)} copy(bf16[32,2,256,128]{3,2,1,0:T(8,128)(2,1)} %stack.1) | data formatting | bytes 8388608

commit v4 on v3

--- a/solution.py
+++ b/solution.py
@@ -11,6 +11,7 @@
 BF = jnp.bfloat16
 F32 = jnp.float32
 GROUP = 4
+BATCH = 8
 
 
 def cat(parts, axis):
@@ -57,17 +58,19 @@
 
 
 def body(
-    dims, img, w_a_hbm, w_down_hbm, w_in_hbm, w_mid_hbm, w_out_hbm, bn_a, bn_down, bn_in, bn_mid, bn_out, out,
+    dims, img, w_a_hbm, w_down_hbm, w_in_hbm, w_mid_hbm, w_out_hbm, bn_a, bn_down, bn_in, bn_mid, bn_out, hb,
     w_a_raw, w_down_raw, w_in_raw, w_mid_raw, w_out_raw, wa, w4, wd, w_in, w_out, w_mid,
-    xb, halo, za, z4, zb, hb, ub, hh, rb,
+    xb, halo, za, z4, zb, ub, hh, rb,
     msg, pslot, cmsg, slots,
-    ld_sem, im_send, im_recv, ex_send, ex_recv, ar_send, ar_recv, out_sem, w_sem,
+    ld_sem, im_send, im_recv, ex_send, ex_recv, ar_send, ar_recv, w_sem,
 ):
     n_img, width, sp_n, blocks, count_a, count_b = dims
     half = width // 2
     n_grp = n_img // GROUP
     rows = GROUP * half
-    fold = rows // width
+    n_bat = n_img // BATCH
+    rows_b = BATCH * half
+    chunks = BATCH // GROUP
     me = lax.axis_index("sp")
     core = lax.rem(me, 2)
     chip = lax.div(me, 2)
@@ -280,11 +283,15 @@
                 ex_copy(1, g, src, dst, up).wait_send()
 
     def get(ref, part):
-        return cat([ref[0, part].reshape(rows, 128), ref[1, part].reshape(rows, 128)], 1)
+        return cat([ref[r, part].reshape(part.size * half, 128) for r in range(2)], 1)
 
     def put(ref, part, v):
-        ref[0, part] = v[:, :128].reshape(GROUP, half, 128)
-        ref[1, part] = v[:, 128:].reshape(GROUP, half, 128)
+        for r in range(2):
+            ref[r, part] = v[:, r * 128:(r + 1) * 128].reshape(part.size, half, 128)
+
+    def ex_batch(g, src, dst):
+        for c in range(chunks):
+            ex_start(g * chunks + c, src, dst)
 
     lane = lax.broadcasted_iota(jnp.int32, (1, 256), 1)
     valid = ((lane < 128) & has_up) | ((lane >= 128) & has_dn)
@@ -294,8 +301,8 @@
         src, dst = (hb, hh) if j == 0 else (ub, rb)
 
         def conv_in(g, carry):
-            part = pl.ds(g * GROUP, GROUP)
-            z = zb[part].reshape(rows, 256)
+            part = pl.ds(g * BATCH, BATCH)
+            z = zb[part].reshape(rows_b, 256)
             if j == 0:
                 h = norm(z, m_prev).astype(BF)
             else:
@@ -304,15 +311,18 @@
             if j == 0:
                 @pl.when(g > 0)
                 def _():
-                    ex_start(g - 1, src, dst)
+                    ex_batch(g - 1, src, dst)
             z = dot(h, w_in[j])
-            zb[part] = z.reshape(GROUP, half, 256)
+            zb[part] = z.reshape(BATCH, half, 256)
             return add_stats(carry, z)
 
-        stats = lax.fori_loop(0, n_grp, conv_in, zero_stats)
+        stats = lax.fori_loop(0, n_bat, conv_in, zero_stats)
         if j == 0:
-            ex_start(n_grp - 1, src, dst)
-        def prep(g, slot):
+            ex_batch(n_bat - 1, src, dst)
+
+        m_in = moments(2 + 3 * j, stats, count_b, bn_in[j])
+
+        def conv_mid(g, carry):
             part = pl.ds(g * GROUP, GROUP)
 
             @pl.when(has_up)
@@ -329,71 +339,47 @@
                 h = jnp.maximum((z - m_prev[0]) * m_prev[1] + m_prev[2] + h.astype(F32), 0.0).astype(BF)
                 if j < blocks - 1:
                     put(hh, part, h)
-            z = dot(h, w_in[j])
-            for c in range(2):
-                za[c, pl.ds(slot * fold, fold)] = z[:, c * 128:(c + 1) * 128].reshape(fold, width, 128)
-
-        def main(g, slot, carry):
-            part = pl.ds(g * GROUP, GROUP)
-            zh = cat([za[c, pl.ds(slot * fold, fold)].reshape(rows, 128) for c in range(2)], 1)
+            zh = dot(h, w_in[j])
             u = norm(zb[part].reshape(rows, 256), m_in).astype(BF)
+            z = dot(shifts(u, half), w_mid[j, :768])
             v = jnp.where(valid, norm(zh, m_in), 0.0).astype(BF)
-            z = dot(cat([shifts(u, half), shifts(v, half)], 1), w_mid[j])
+            z = z + dot(shifts(v, half), w_mid[j, 768:])
             zb[part] = z.reshape(GROUP, half, 256)
             return add_stats(carry, z)
 
-        m_in = moments(2 + 3 * j, stats, count_b, bn_in[j], meanwhile=lambda: prep(0, 0))
-
-        def conv_mid(i, carry):
-            prep(2 * i + 1, 1)
-            carry = main(2 * i, 0, carry)
-            prep(2 * i + 2, 0)
-            return main(2 * i + 1, 1, carry)
-
-        stats = lax.fori_loop(0, n_grp // 2 - 1, conv_mid, zero_stats)
-        prep(n_grp - 1, 1)
-        stats = main(n_grp - 1, 1, main(n_grp - 2, 0, stats))
+        stats = lax.fori_loop(0, n_grp, conv_mid, zero_stats)
         ex_wait_send(src, dst)
         m_mid = moments(3 + 3 * j, stats, count_b, bn_mid[j])
 
         def conv_out(g, carry):
-            part = pl.ds(g * GROUP, GROUP)
-            u = norm(zb[part].reshape(rows, 256), m_mid).astype(BF)
+            part = pl.ds(g * BATCH, BATCH)
+            u = norm(zb[part].reshape(rows_b, 256), m_mid).astype(BF)
             if j < blocks - 1:
                 put(ub, part, u)
 
                 @pl.when(g > 0)
                 def _():
-                    ex_start(g - 1, ub, rb)
+                    ex_batch(g - 1, ub, rb)
             z = dot(u, w_out[j])
-            zb[part] = z.reshape(GROUP, half, 256)
+            zb[part] = z.reshape(BATCH, half, 256)
             return add_stats(carry, z)
 
-        stats = lax.fori_loop(0, n_grp, conv_out, zero_stats)
+        stats = lax.fori_loop(0, n_bat, conv_out, zero_stats)
         if j < blocks - 1:
-            ex_start(n_grp - 1, ub, rb)
+            ex_batch(n_bat - 1, ub, rb)
         m = moments(4 + 3 * j, stats, count_b, bn_out[j])
 
-    def out_copy(g, r):
-        part = pl.ds(g * GROUP, GROUP)
-        return pltpu.make_async_copy(hb.at[r, part], out.at[part, r], out_sem.at[r, g])
-
     def finish(g, carry):
-        part = pl.ds(g * GROUP, GROUP)
-        z = zb[part].reshape(rows, 256)
+        part = pl.ds(g * BATCH, BATCH)
+        z = zb[part].reshape(rows_b, 256)
         h = jnp.maximum((z - m[0]) * m[1] + m[2] + get(hb, part).astype(F32), 0.0).astype(BF)
         put(hb, part, h)
-        for r in range(2):
-            out_copy(g, r).start()
         return carry
 
-    lax.fori_loop(0, n_grp, finish, 0)
+    lax.fori_loop(0, n_bat, finish, 0)
 
     @pl.loop(0, n_grp)
     def _(g):
-        for r in range(2):
-            out_copy(g, r).wait()
-
         @pl.when(has_dn)
         def _():
             img_copy(0, g, dn).wait_send()
@@ -429,11 +415,11 @@
         vmem = pl.BlockSpec(memory_space=pltpu.VMEM)
         anys = pl.BlockSpec(memory_space=pl.ANY)
         plane = (2, n_img, half, 128)
-        return pl.pallas_call(
+        rows_first = pl.pallas_call(
             functools.partial(body, dims),
-            out_shape=jax.ShapeDtypeStruct((n_img, rows_dev // 2, half, 128), BF),
+            out_shape=pltpu.VMEM(plane, BF),
             in_specs=[anys] * 6 + [vmem] * 5,
-            out_specs=anys,
+            out_specs=vmem,
             scratch_shapes=[
                 pltpu.VMEM(w_a.shape, BF),
                 pltpu.VMEM(w_down.shape, BF),
@@ -454,7 +440,6 @@
                 pltpu.VMEM(plane, BF),
                 pltpu.VMEM(plane, BF),
                 pltpu.VMEM(plane, BF),
-                pltpu.VMEM(plane, BF),
                 pltpu.VMEM((n_bn, 16, 128), F32),
                 pltpu.VMEM((n_bn, 16, 128), F32),
                 pltpu.VMEM((n_bn, 16, 128), F32),
@@ -466,13 +451,13 @@
                 pltpu.SemaphoreType.DMA((2, n_grp)),
                 pltpu.SemaphoreType.DMA((n_bn, 5)),
                 pltpu.SemaphoreType.DMA((n_bn, 4)),
-                pltpu.SemaphoreType.DMA((2, n_grp)),
                 pltpu.SemaphoreType.DMA((5,)),
             ],
             compiler_params=pltpu.CompilerParams(
-                collective_id=0, has_side_effects=True, vmem_limit_bytes=67043328),
+                collective_id=0, has_side_effects=True, vmem_limit_bytes=67043328 - 2 * n_img * half * 128 * 2),
             name="stack",
         )(x, w_a, w_down, w_in, w_mid, w_out, bn_a, bn_down, bn_in, bn_mid, bn_out)
+        return jnp.transpose(rows_first, (1, 0, 2, 3))
 
     act_spec = P("dp", "sp", None, None)
     return jax.shard_map(forward, mesh=mesh, in_specs=(act_spec,) + (P(),) * 10, out_specs=act_spec, check_vma=False)

time: 183 us -> 173 us (0.945)
  Pallas kernels: 178 us -> 171 us
  local copies, waits for them, and re-layouts: 4.7 us -> 2.51 us
    pallas_call x1, Pallas kernels: 178 us -> 171 us  [forward(): pl.pallas_call(functools.partial(body, dims), out_shape=pltpu.VMEM(plane,...]
    unnamed x1 -> x0, local copies, waits for them, and re-layouts: 4.7 us -> none
    transpose x0 -> x1, local copies, waits for them, and re-layouts: none -> 2.51 us  [forward(): return jnp.transpose(rows_first, (1, 0, 2, 3))]
where the time goes in v4:
time: 173 us
  Pallas kernels  171 us (99%)
  local copies, waits for them, and re-layouts  2.51 us (1%)
    pallas_call x1, Pallas kernels, forward(): pl.pallas_call(functools.partial(body, dims), out_shape=pltpu.VMEM(plane,...  171 us

profile of v4, /device:TPU:81, one launch (start us, length us, event | category | flops | bytes accessed | tf_op | source)
XLA Modules:
  0.0 173.4 jit_solution(7396923534005823024)
XLA Ops:
  0.0 170.8 %stack.1 = bf16[2,32,256,128]{3,2,1,0:T(8,128)(2,1)S(1)} custom-call(bf16[32,4,64,512]{3,2,1,0:T(8,128)(2,1)} %bitcast.3, bf16[1,3,3,64,64]{4,3,2,1,0:T(8,128)(2,1)} %w_a_hbm.1, bf16[3,3,64,128]{3,2,1,0:T(8,128)(2,1)} %w_down_hbm.1, bf16[3,128,128]{2,1,0:T(8,128)(2,1)} %w_in_hbm.1, bf16[3,3,3,128,128]{4,3,2,1,0:T(8,128)(2,1)} %w_mid_hbm.1, ...), custom_call_target="tpu_custom_call" | custom-call | tf_op jit(solution)/shard_map/stack/pallas_call | solution.py:418
  170.9 2.5 %copy.12 = bf16[32,2,256,128]{3,2,1,0:T(8,128)(2,1)} copy(bf16[32,2,256,128]{3,2,0,1:T(8,128)(2,1)S(1)} %bitcast.2) | data formatting | bytes 8388608 | tf_op jit(solution)/shard_map/transpose | solution.py:460

commit v5 on v4

--- a/solution.py
+++ b/solution.py
@@ -11,6 +11,7 @@
 BF = jnp.bfloat16
 F32 = jnp.float32
 GROUP = 4
+LATE = 1
 BATCH = 8
 
 
@@ -62,12 +63,13 @@
     w_a_raw, w_down_raw, w_in_raw, w_mid_raw, w_out_raw, wa, w4, wd, w_in, w_out, w_mid,
     xb, halo, za, z4, zb, ub, hh, rb,
     msg, pslot, cmsg, slots,
-    ld_sem, im_send, im_recv, ex_send, ex_recv, ar_send, ar_recv, w_sem,
+    ld_sem, im_send, im_recv, ex_send, ex_recv, ar_send, ar_recv, w_sem, all8, d_send, d_recv,
 ):
     n_img, width, sp_n, blocks, count_a, count_b = dims
     half = width // 2
     n_grp = n_img // GROUP
     rows = GROUP * half
+    fold = rows // width
     n_bat = n_img // BATCH
     rows_b = BATCH * half
     chunks = BATCH // GROUP
@@ -97,6 +99,8 @@
 
     load(0).start()
 
+    direct_ks = [1] + [3 + 3 * j for j in range(blocks)] + [1 + 3 * blocks]
+
     bar = pltpu.get_barrier_semaphore()
     for k in range(1, sp_n):
         pl.semaphore_signal(bar, inc=1, device_id={"sp": lax.rem(me + k, sp_n)}, device_id_type=pl.DeviceIdType.MESH)
@@ -153,32 +157,48 @@
     def norm(z, m):
         return jnp.maximum((z - m[0]) * m[1] + m[2], 0.0)
 
+    def direct(d, other):
+        return remote(msg.at[direct_ks[d]], all8.at[d, me], d_send.at[d, other], d_recv.at[d, me], other)
+
     def moments(k, stats, count, p, fold64=False, meanwhile=None):
         s, q = (t[:, :128] + t[:, 128:] for t in stats)
         if fold64:
             s, q = s + pltpu.roll(s, 64, 1), q + pltpu.roll(q, 64, 1)
         own = cat([s, q], 0)
         msg[k] = own
-        first = remote(msg.at[k], pslot.at[k], ar_send.at[k, 0], ar_recv.at[k, 3], me + 1 - 2 * core)
-        first.start()
-        first.wait_recv()
-        mine = own + pslot[k]
-        cmsg[k] = mine
-        near = lax.rem(chip + 1 + core * (chips - 2), chips)
-        far = lax.rem(chip + 2, chips)
-        for c in range(2):
-            remote(cmsg.at[k], slots.at[k, core], ar_send.at[k, 1 + c], ar_recv.at[k, core], near * 2 + c).start()
-
-        @pl.when(core == lax.rem(chip, 2))
-        def _():
+        if k in direct_ks:
+            d = direct_ks.index(k)
+            all8[d, me] = own
+            for i in range(1, sp_n):
+                direct(d, lax.rem(me + i, sp_n)).start()
+            for i in range(1, sp_n):
+                other = lax.rem(me + i, sp_n)
+                remote(msg.at[k], all8.at[d, other], d_send.at[d, other], d_recv.at[d, other], other).wait_recv()
+            parts = [all8[d, i] for i in range(sp_n)]
+            while len(parts) > 1:
+                parts = [parts[i] + parts[i + 1] for i in range(0, len(parts), 2)]
+            tot = parts[0]
+        else:
+            first = remote(msg.at[k], pslot.at[k], ar_send.at[k, 0], ar_recv.at[k, 3], me + 1 - 2 * core)
+            first.start()
+            first.wait_recv()
+            mine = own + pslot[k]
+            cmsg[k] = mine
+            near = lax.rem(chip + 1 + core * (chips - 2), chips)
+            far = lax.rem(chip + 2, chips)
             for c in range(2):
-                remote(cmsg.at[k], slots.at[k, 2], ar_send.at[k, 3 + c], ar_recv.at[k, 2], far * 2 + c).start()
-
-        if meanwhile is not None:
-            meanwhile()
-        for c in range(3):
-            remote(cmsg.at[k], slots.at[k, c], ar_send.at[k, 1], ar_recv.at[k, c], me).wait_recv()
-        tot = (mine + slots[k, 2]) + (slots[k, 0] + slots[k, 1])
+                remote(cmsg.at[k], slots.at[k, core], ar_send.at[k, 1 + c], ar_recv.at[k, core], near * 2 + c).start()
+
+            @pl.when(core == lax.rem(chip, 2))
+            def _():
+                for c in range(2):
+                    remote(cmsg.at[k], slots.at[k, 2], ar_send.at[k, 3 + c], ar_recv.at[k, 2], far * 2 + c).start()
+
+            if meanwhile is not None:
+                meanwhile()
+            for c in range(3):
+                remote(cmsg.at[k], slots.at[k, c], ar_send.at[k, 1], ar_recv.at[k, c], me).wait_recv()
+            tot = (mine + slots[k, 2]) + (slots[k, 0] + slots[k, 1])
         inv = 1.0 / count
         mean = jnp.sum(tot[:8], axis=0, keepdims=True) * inv
         var = jnp.sum(tot[8:], axis=0, keepdims=True) * inv - mean * mean
@@ -320,18 +340,16 @@
         if j == 0:
             ex_batch(n_bat - 1, src, dst)
 
-        m_in = moments(2 + 3 * j, stats, count_b, bn_in[j])
-
-        def conv_mid(g, carry):
-            part = pl.ds(g * GROUP, GROUP)
-
-            @pl.when(has_up)
-            def _():
-                ex_copy(0, g, src, dst, dn).wait_recv()
-
-            @pl.when(has_dn)
-            def _():
-                ex_copy(1, g, src, dst, up).wait_recv()
+        def halo_rows(g, many):
+            part = pl.ds(g * GROUP * many, GROUP * many)
+            for c in range(many):
+                @pl.when(has_up)
+                def _():
+                    ex_copy(0, g * many + c, src, dst, dn).wait_recv()
+
+                @pl.when(has_dn)
+                def _():
+                    ex_copy(1, g * many + c, src, dst, up).wait_recv()
 
             h = get(hh, part)
             if j > 0:
@@ -339,15 +357,38 @@
                 h = jnp.maximum((z - m_prev[0]) * m_prev[1] + m_prev[2] + h.astype(F32), 0.0).astype(BF)
                 if j < blocks - 1:
                     put(hh, part, h)
-            zh = dot(h, w_in[j])
-            u = norm(zb[part].reshape(rows, 256), m_in).astype(BF)
+            return dot(h, w_in[j])
+
+        def taps(g, many, zh, carry):
+            images = GROUP * many
+            part = pl.ds(g * images, images)
+            u = norm(zb[part].reshape(images * half, 256), m_in).astype(BF)
             z = dot(shifts(u, half), w_mid[j, :768])
             v = jnp.where(valid, norm(zh, m_in), 0.0).astype(BF)
             z = z + dot(shifts(v, half), w_mid[j, 768:])
-            zb[part] = z.reshape(GROUP, half, 256)
+            zb[part] = z.reshape(images, half, 256)
             return add_stats(carry, z)
 
-        stats = lax.fori_loop(0, n_grp, conv_mid, zero_stats)
+        def conv_mid(g, carry, many):
+            return taps(g, many, halo_rows(g, many), carry)
+
+        def first_pair():
+            @pl.loop(0, 2)
+            def _(g):
+                zh = halo_rows(g, 1)
+                for c in range(2):
+                    za[c, pl.ds(g * fold, fold)] = zh[:, c * 128:(c + 1) * 128].reshape(fold, width, 128)
+
+        m_in = moments(2 + 3 * j, stats, count_b, bn_in[j], meanwhile=first_pair)
+
+        def prepared(g, carry):
+            zh = cat([za[c, pl.ds(g * fold, fold)].reshape(rows, 128) for c in range(2)], 1)
+            return taps(g, 1, zh, carry)
+
+        stats = lax.fori_loop(0, 2, prepared, zero_stats)
+
+        stats = lax.fori_loop(1, n_grp // 2 - LATE, functools.partial(conv_mid, many=2), stats)
+        stats = lax.fori_loop(n_grp - 2 * LATE, n_grp, functools.partial(conv_mid, many=1), stats)
         ex_wait_send(src, dst)
         m_mid = moments(3 + 3 * j, stats, count_b, bn_mid[j])
 
@@ -389,8 +430,13 @@
             img_copy(1, g, up).wait_send()
             img_copy(2, g, up).wait_send()
 
-    @pl.loop(0, 2 + 3 * blocks)
-    def _(k):
+    for k in range(2 + 3 * blocks):
+        if k in direct_ks:
+            d = direct_ks.index(k)
+            for i in range(1, sp_n):
+                direct(d, lax.rem(me + i, sp_n)).wait_send()
+            continue
+
         remote(msg.at[k], pslot.at[k], ar_send.at[k, 0], ar_recv.at[k, 3], me).wait_send()
         for c in range(2):
             remote(cmsg.at[k], slots.at[k, 0], ar_send.at[k, 1 + c], ar_recv.at[k, 0], me).wait_send()
@@ -452,6 +498,9 @@
                 pltpu.SemaphoreType.DMA((n_bn, 5)),
                 pltpu.SemaphoreType.DMA((n_bn, 4)),
                 pltpu.SemaphoreType.DMA((5,)),
+                pltpu.VMEM((2 + blocks, sp_n, 16, 128), F32),
+                pltpu.SemaphoreType.DMA((2 + blocks, sp_n)),
+                pltpu.SemaphoreType.DMA((2 + blocks, sp_n)),
             ],
             compiler_params=pltpu.CompilerParams(
                 collective_id=0, has_side_effects=True, vmem_limit_bytes=67043328 - 2 * n_img * half * 128 * 2),

time: 173 us -> 167 us (0.965)
  Pallas kernels: 171 us -> 165 us
    pallas_call x1, Pallas kernels: 171 us -> 165 us  [forward(): pl.pallas_call(functools.partial(body, dims), out_shape=pltpu.VMEM(plane,...]
where the time goes in v5:
time: 167 us
  Pallas kernels  165 us (99%)
  local copies, waits for them, and re-layouts  2.51 us (2%)
    pallas_call x1, Pallas kernels, forward(): pl.pallas_call(functools.partial(body, dims), out_shape=pltpu.VMEM(plane,...  165 us

profile of v5, /device:TPU:81, one launch (start us, length us, event | category | flops | bytes accessed | tf_op | source)
XLA Modules:
  0.0 167.3 jit_solution(7611164160668692770)
XLA Ops:
  0.0 164.7 %stack.1 = bf16[2,32,256,128]{3,2,1,0:T(8,128)(2,1)S(1)} custom-call(bf16[32,4,64,512]{3,2,1,0:T(8,128)(2,1)} %bitcast.3, bf16[1,3,3,64,64]{4,3,2,1,0:T(8,128)(2,1)} %w_a_hbm.1, bf16[3,3,64,128]{3,2,1,0:T(8,128)(2,1)} %w_down_hbm.1, bf16[3,128,128]{2,1,0:T(8,128)(2,1)} %w_in_hbm.1, bf16[3,3,3,128,128]{4,3,2,1,0:T(8,128)(2,1)} %w_mid_hbm.1, ...), custom_call_target="tpu_custom_call" | custom-call | tf_op jit(solution)/shard_map/stack/pallas_call | solution.py:464
  164.7 2.5 %copy.12 = bf16[32,2,256,128]{3,2,1,0:T(8,128)(2,1)} copy(bf16[32,2,256,128]{3,2,0,1:T(8,128)(2,1)S(1)} %bitcast.2) | data formatting | bytes 8388608 | tf_op jit(solution)/shard_map/transpose | solution.py:509

commit v6 on v5

--- a/solution.py
+++ b/solution.py
@@ -164,12 +164,12 @@
         s, q = (t[:, :128] + t[:, 128:] for t in stats)
         if fold64:
             s, q = s + pltpu.roll(s, 64, 1), q + pltpu.roll(q, 64, 1)
-        own = cat([s, q], 0)
+        own = cat([jnp.sum(s, axis=0, keepdims=True), jnp.sum(q, axis=0, keepdims=True), jnp.zeros((6, 128), F32)], 0)
         msg[k] = own
         if k in direct_ks:
             d = direct_ks.index(k)
             all8[d, me] = own
-            for i in range(1, sp_n):
+            for i in sorted(range(1, sp_n), key=lambda i: abs(i - chips)):
                 direct(d, lax.rem(me + i, sp_n)).start()
             for i in range(1, sp_n):
                 other = lax.rem(me + i, sp_n)
@@ -186,13 +186,13 @@
             cmsg[k] = mine
             near = lax.rem(chip + 1 + core * (chips - 2), chips)
             far = lax.rem(chip + 2, chips)
-            for c in range(2):
-                remote(cmsg.at[k], slots.at[k, core], ar_send.at[k, 1 + c], ar_recv.at[k, core], near * 2 + c).start()
-
             @pl.when(core == lax.rem(chip, 2))
             def _():
                 for c in range(2):
                     remote(cmsg.at[k], slots.at[k, 2], ar_send.at[k, 3 + c], ar_recv.at[k, 2], far * 2 + c).start()
+
+            for c in range(2):
+                remote(cmsg.at[k], slots.at[k, core], ar_send.at[k, 1 + c], ar_recv.at[k, core], near * 2 + c).start()
 
             if meanwhile is not None:
                 meanwhile()
@@ -200,8 +200,8 @@
                 remote(cmsg.at[k], slots.at[k, c], ar_send.at[k, 1], ar_recv.at[k, c], me).wait_recv()
             tot = (mine + slots[k, 2]) + (slots[k, 0] + slots[k, 1])
         inv = 1.0 / count
-        mean = jnp.sum(tot[:8], axis=0, keepdims=True) * inv
-        var = jnp.sum(tot[8:], axis=0, keepdims=True) * inv - mean * mean
+        mean = tot[0:1] * inv
+        var = tot[1:2] * inv - mean * mean
         scale = p[0:1] * lax.rsqrt(var + NORM_EPS)
         return tuple(cat([t, t], 1) for t in (mean, scale, p[1:2]))
 
@@ -486,10 +486,10 @@
                 pltpu.VMEM(plane, BF),
                 pltpu.VMEM(plane, BF),
                 pltpu.VMEM(plane, BF),
-                pltpu.VMEM((n_bn, 16, 128), F32),
-                pltpu.VMEM((n_bn, 16, 128), F32),
-                pltpu.VMEM((n_bn, 16, 128), F32),
-                pltpu.VMEM((n_bn, 3, 16, 128), F32),
+                pltpu.VMEM((n_bn, 8, 128), F32),
+                pltpu.VMEM((n_bn, 8, 128), F32),
+                pltpu.VMEM((n_bn, 8, 128), F32),
+                pltpu.VMEM((n_bn, 3, 8, 128), F32),
                 pltpu.SemaphoreType.DMA((2,)),
                 pltpu.SemaphoreType.DMA((3, n_grp)),
                 pltpu.SemaphoreType.DMA((3, n_grp)),
@@ -498,7 +498,7 @@
                 pltpu.SemaphoreType.DMA((n_bn, 5)),
                 pltpu.SemaphoreType.DMA((n_bn, 4)),
                 pltpu.SemaphoreType.DMA((5,)),
-                pltpu.VMEM((2 + blocks, sp_n, 16, 128), F32),
+                pltpu.VMEM((2 + blocks, sp_n, 8, 128), F32),
                 pltpu.SemaphoreType.DMA((2 + blocks, sp_n)),
                 pltpu.SemaphoreType.DMA((2 + blocks, sp_n)),
             ],

time: 167 us -> 164 us (0.982)
  Pallas kernels: 165 us -> 161 us
    pallas_call x1, Pallas kernels: 165 us -> 161 us  [forward(): pl.pallas_call(functools.partial(body, dims), out_shape=pltpu.VMEM(plane,...]
where the time goes in v6:
time: 164 us
  Pallas kernels  161 us (98%)
  local copies, waits for them, and re-layouts  2.51 us (2%)
    pallas_call x1, Pallas kernels, forward(): pl.pallas_call(functools.partial(body, dims), out_shape=pltpu.VMEM(plane,...  161 us

profile of v6, /device:TPU:81, one launch (start us, length us, event | category | flops | bytes accessed | tf_op | source)
XLA Modules:
  0.0 163.8 jit_solution(12216562984917813682)
XLA Ops:
  0.0 161.2 %stack.1 = bf16[2,32,256,128]{3,2,1,0:T(8,128)(2,1)S(1)} custom-call(bf16[32,4,64,512]{3,2,1,0:T(8,128)(2,1)} %bitcast.3, bf16[1,3,3,64,64]{4,3,2,1,0:T(8,128)(2,1)} %w_a_hbm.1, bf16[3,3,64,128]{3,2,1,0:T(8,128)(2,1)} %w_down_hbm.1, bf16[3,128,128]{2,1,0:T(8,128)(2,1)} %w_in_hbm.1, bf16[3,3,3,128,128]{4,3,2,1,0:T(8,128)(2,1)} %w_mid_hbm.1, ...), custom_call_target="tpu_custom_call" | custom-call | tf_op jit(solution)/shard_map/stack/pallas_call | solution.py:464
  161.2 2.5 %copy.12 = bf16[32,2,256,128]{3,2,1,0:T(8,128)(2,1)} copy(bf16[32,2,256,128]{3,2,0,1:T(8,128)(2,1)S(1)} %bitcast.2) | data formatting | bytes 8388608 | tf_op jit(solution)/shard_map/transpose | solution.py:509

commit v7 on v6

--- a/solution.py
+++ b/solution.py
@@ -320,9 +320,11 @@
         m_prev = m
         src, dst = (hb, hh) if j == 0 else (ub, rb)
 
+        batch = GROUP if j == 0 else BATCH
+
         def conv_in(g, carry):
-            part = pl.ds(g * BATCH, BATCH)
-            z = zb[part].reshape(rows_b, 256)
+            part = pl.ds(g * batch, batch)
+            z = zb[part].reshape(batch * half, 256)
             if j == 0:
                 h = norm(z, m_prev).astype(BF)
             else:
@@ -331,14 +333,14 @@
             if j == 0:
                 @pl.when(g > 0)
                 def _():
-                    ex_batch(g - 1, src, dst)
+                    ex_start(g - 1, src, dst)
             z = dot(h, w_in[j])
-            zb[part] = z.reshape(BATCH, half, 256)
+            zb[part] = z.reshape(batch, half, 256)
             return add_stats(carry, z)
 
-        stats = lax.fori_loop(0, n_bat, conv_in, zero_stats)
+        stats = lax.fori_loop(0, n_img // batch, conv_in, zero_stats)
         if j == 0:
-            ex_batch(n_bat - 1, src, dst)
+            ex_start(n_grp - 1, src, dst)
 
         def halo_rows(g, many):
             part = pl.ds(g * GROUP * many, GROUP * many)

time: 164 us -> 163 us (level)
  no operation moved by 1% of the time
where the time goes in v7:
time: 163 us
  Pallas kernels  161 us (99%)
  local copies, waits for them, and re-layouts  2.51 us (2%)
    pallas_call x1, Pallas kernels, forward(): pl.pallas_call(functools.partial(body, dims), out_shape=pltpu.VMEM(plane,...  161 us

profile of v7, /device:TPU:81, one launch (start us, length us, event | category | flops | bytes accessed | tf_op | source)
XLA Modules:
  0.0 163.2 jit_solution(13124215425993634808)
XLA Ops:
  0.0 160.7 %stack.1 = bf16[2,32,256,128]{3,2,1,0:T(8,128)(2,1)S(1)} custom-call(bf16[32,4,64,512]{3,2,1,0:T(8,128)(2,1)} %bitcast.3, bf16[1,3,3,64,64]{4,3,2,1,0:T(8,128)(2,1)} %w_a_hbm.1, bf16[3,3,64,128]{3,2,1,0:T(8,128)(2,1)} %w_down_hbm.1, bf16[3,128,128]{2,1,0:T(8,128)(2,1)} %w_in_hbm.1, bf16[3,3,3,128,128]{4,3,2,1,0:T(8,128)(2,1)} %w_mid_hbm.1, ...), custom_call_target="tpu_custom_call" | custom-call | tf_op jit(solution)/shard_map/stack/pallas_call | solution.py:466
  160.7 2.5 %copy.12 = bf16[32,2,256,128]{3,2,1,0:T(8,128)(2,1)} copy(bf16[32,2,256,128]{3,2,0,1:T(8,128)(2,1)S(1)} %bitcast.2) | data formatting | bytes 8388608 | tf_op jit(solution)/shard_map/transpose | solution.py:511
